TPU v7x, 32 devices: a whole 2x2x4 slice. The times are simulated.
32 devices in a mesh: group: 4 (over y, core), member: 8 (over z, x).
Axes of the slice: x: 2, y: 2, z: 4, core: 2. Of those that a mesh axis runs over, the one named last changes fastest.
Arguments:
- off_tiles: bfloat16 [64, 8, 128, 128], P(('group', 'member')), may hold values from -0.1875 to 0.1875
- off_cols: int32 [64, 8], P(('group', 'member')), may hold values from 0 to 17
- member_send: int32 [32, 8, 1], P(('group', 'member')), may hold values from 0 to 1
- group_send: int32 [32, 4], P(('group', 'member')), may hold values from 0 to 1
- diag_tiles: bfloat16 [64, 128, 128], P(('group', 'member')), may hold values from -1 to 9
- smoother: bfloat16 [64, 128, 128], P(('group', 'member')), may hold values from -1 to 1
- agg_map: int32 [64], P(('group', 'member')), may hold values from 0 to 1
- prolong: bfloat16 [64, 128, 128], P(('group', 'member')), may hold values from -0.5 to 0.5
- coarse_inv: bfloat16 [1024, 1024], P(None, 'group'), may hold values from -0.03125 to 0.03125
- krylov_basis: bfloat16 [64, 32, 128], P(('group', 'member')), may hold values from -24 to 24, as said below
Outputs:
- preconditioned: bfloat16 [64, 8, 128], P(('group', 'member'))
- coefficients: float32 [32, 8], replicated
- gram_matrix: float32 [8, 8], replicated
- new_block: float32 [64, 8, 128], P(('group', 'member'))
Inputs may be any that keep to these rules, and one draw needn't show every extreme that they name: `off_cols`: entries below 2 name the device's own row tiles; entry 2 + p + s names slot s of what member p of the same group sends; the last 8 entries name what the groups below and above send. `member_send`: entry [d, p, s] is the local row tile that device d sends to member p of its group in slot s. `group_send`: entry [d, s] is the local row tile that device d sends, in slot s, to the same member of the groups below and above. `krylov_basis`: the 32 basis vectors are orthonormal, up to bfloat16 rounding, under the inner product (1 / 8192) times the sum over all rows.
All inputs are finite; a program needn't handle non-finite values.
Results may differ from a plain program's by a relative error of at most 0.02.
Values may be sent and summed in bfloat16 or wider, within the bound.
No kernel may reach another device: no remote copies, remote signals or barrier semaphores. Data moves between devices by JAX's collectives and lax.ppermute only.
A program may use at most 64 MiB of HBM per device.

v0:
```python
import jax
import jax.numpy as jnp
from jax import lax
from jax.sharding import PartitionSpec as P

TILE = 128
NVEC = 8
GH = 1
CTG = 2


def extended_2(cells, sides, width):
    for axis, dim in sides:
        count = lax.axis_size(axis)
        ends = count - 1
        head = lax.slice_in_dim(cells, 0, width, axis=dim)
        tail = lax.slice_in_dim(cells, cells.shape[dim] - width, cells.shape[dim], axis=dim)
        cells = jnp.concatenate(
            [
                lax.ppermute(tail, axis, [(i, (i + 1) % count) for i in range(ends)]),
                cells,
                lax.ppermute(head, axis, [((i + 1) % count, i) for i in range(ends)]),
            ],
            axis=dim,
        )
    return cells


def extend_tiles(values, member_send, group_send, members):
    outgoing = values[member_send[0].reshape(-1)].reshape(members, GH, NVEC, TILE)
    arrived = lax.all_to_all(outgoing, "member", split_axis=0, concat_axis=0, tiled=True).reshape(
        members * GH, NVEC, TILE
    )
    rim_tiles = values[group_send[0]][None]
    beside = extended_2(rim_tiles, (("group", 0),), 1)
    return jnp.concatenate([values, arrived, beside[0], beside[2]], axis=0)


def operate(values, off_tiles, off_cols, diag_tiles, member_send, group_send, members):
    extended = extend_tiles(values, member_send, group_send, members)
    picked = extended[off_cols]
    far_part = jnp.einsum("tkcj,tkji->tci", picked, off_tiles, preferred_element_type=jnp.float32)
    near_part = jnp.einsum("tcj,tji->tci", values, diag_tiles, preferred_element_type=jnp.float32)
    return near_part + far_part


def tilewise(left_side, tiles):
    return jnp.einsum("tcj,tji->tci", left_side, tiles, preferred_element_type=jnp.float32)


def exact_product(form, first_operand, second_operand):
    return jnp.einsum(form, first_operand, second_operand, precision=lax.Precision.HIGHEST)


def local(
    off_tiles,
    off_cols,
    member_send,
    group_send,
    diag_tiles,
    smoother,
    agg_map,
    prolong,
    coarse_inv,
    krylov_basis,
):
    members = lax.axis_size("member")
    groups = lax.axis_size("group")
    tiles_dev = diag_tiles.shape[0]
    rows_all = tiles_dev * TILE * members * groups
    scale_rows = 1.0 / rows_all

    def apply_operator(values):
        return operate(values, off_tiles, off_cols, diag_tiles, member_send, group_send, members)

    last_block = krylov_basis[:, krylov_basis.shape[1] - NVEC :, :]
    block_wide = last_block.astype(jnp.float32)
    first = tilewise(last_block, smoother).astype(jnp.bfloat16)
    residual_one = (block_wide - apply_operator(first)).astype(jnp.bfloat16)
    pieces = jnp.einsum("tci,tji->tcj", residual_one, prolong, preferred_element_type=jnp.float32)
    selector = (agg_map[:, None] == jnp.arange(CTG, dtype=jnp.int32)[None, :]).astype(jnp.float32)
    coarse_part = exact_product("ta,tcj->acj", selector, pieces)
    spread = jnp.zeros((groups, CTG, NVEC, TILE), jnp.float32)
    spread = lax.dynamic_update_slice(spread, coarse_part[None], (lax.axis_index("group"), 0, 0, 0))
    coarse_all = lax.psum(spread, ("group", "member")).reshape(groups * CTG, NVEC, TILE)
    coarse_round = coarse_all.astype(jnp.bfloat16)
    columns = coarse_inv.reshape(groups * CTG, TILE, CTG * TILE)
    correction = jnp.einsum(
        "acj,ajo->co", coarse_round, columns, preferred_element_type=jnp.float32
    )
    correction = correction.astype(jnp.bfloat16).reshape(NVEC, CTG, TILE)
    chosen = jnp.einsum(
        "ta,cak->tck", selector.astype(jnp.bfloat16), correction, preferred_element_type=jnp.float32
    )
    second = (first.astype(jnp.float32) + tilewise(chosen.astype(jnp.bfloat16), prolong)).astype(
        jnp.bfloat16
    )
    residual_two = (block_wide - apply_operator(second)).astype(jnp.bfloat16)
    preconditioned = (second.astype(jnp.float32) + tilewise(residual_two, smoother)).astype(
        jnp.bfloat16
    )
    applied = apply_operator(preconditioned).astype(jnp.bfloat16)
    coeff_part = (
        jnp.einsum("tpi,tci->pc", krylov_basis, applied, preferred_element_type=jnp.float32)
        * scale_rows
    )
    basis_wide = krylov_basis.astype(jnp.float32)
    self_part = (
        jnp.einsum("tci,tdi->cd", applied, applied, preferred_element_type=jnp.float32) * scale_rows
    )
    basis_part = (
        jnp.einsum("tpi,tqi->pq", krylov_basis, krylov_basis, preferred_element_type=jnp.float32)
        * scale_rows
    )
    coefficients, self_total, basis_total = lax.psum(
        (coeff_part, self_part, basis_part), ("group", "member")
    )
    remainder = applied.astype(jnp.float32) - exact_product("pc,tpi->tci", coefficients, basis_wide)
    cross = exact_product("pc,pd->cd", coefficients, coefficients)
    weighted = exact_product("pq,qd->pd", basis_total, coefficients)
    gram_matrix = self_total - 2.0 * cross + exact_product("pc,pd->cd", coefficients, weighted)
    factor = jnp.linalg.cholesky(gram_matrix)
    inverse = lax.linalg.triangular_solve(
        factor, jnp.eye(NVEC, dtype=jnp.float32), left_side=True, lower=True
    )
    new_block = exact_product("cd,tdi->tci", inverse, remainder)
    return (preconditioned, coefficients, gram_matrix, new_block)


def solution(mesh):
    placed = (
        P(("group", "member"), None, None, None),
        P(("group", "member"), None),
        P(("group", "member"), None, None),
        P(("group", "member"), None),
        P(("group", "member"), None, None),
        P(("group", "member"), None, None),
        P(("group", "member")),
        P(("group", "member"), None, None),
        P(None, "group"),
        P(("group", "member"), None, None),
    )
    return jax.shard_map(
        local,
        mesh=mesh,
        in_specs=placed,
        out_specs=(
            P(("group", "member"), None, None),
            P(),
            P(),
            P(("group", "member"), None, None),
        ),
        check_vma=False,
    )
```

profile of v0, /device:TPU:0, one launch (start us, length us, event | category | flops | bytes accessed | tf_op | source)
XLA Modules:
  0.0 144.9 jit_solution(4221777477460338780)
XLA Ops:
  0.6 0.7 fusion.33
  1.4 1.0 convolution_convert_fusion
  2.9 2.4 %collective-permute-start = (bf16[1,4,8,128]{3,2,1,0:T(8,128)(2,1)S(1)}, bf16[1,4,8,128]{3,2,1,0:T(8,128)(2,1)S(1)}, u32[]{:S(2)}, u32[]{:S(2)}) collective-permute-start(bf16[1,4,8,128]{3,2,1,0:T(8,128)(2,1)S(1)} %bitcast.145), channel_id=1, source_target_pairs={{0,8},{8,16},{16,24},{1,9},{9,17},{17,25},{2,10},{10,18},{18,26},{... | collective-permute-start | bytes 24584 | tf_op jit(solution)/shard_map/ppermute | solution.py:20
  5.3 1.3 collective-permute-start.1
  6.7 1.2 gather_fusion
  7.8 6.8 %all-to-all-start = ((bf16[8,1,8,128]{3,2,1,0:T(8,128)(2,1)}), bf16[8,1,8,128]{3,2,1,0:T(8,128)(2,1)S(1)}, u32[]{:S(2)}, u32[]{:S(2)}) async-start(bf16[8,1,8,128]{3,2,1,0:T(8,128)(2,1)} %bitcast.5), calls=%async_computation | async-start | bytes 32768 | tf_op jit(solution)/shard_map/all_to_all | solution.py:31
  14.7 6.5 %all-to-all-done = bf16[8,1,8,128]{3,2,1,0:T(8,128)(2,1)S(1)} async-done(((bf16[8,1,8,128]{3,2,1,0:T(8,128)(2,1)}), bf16[8,1,8,128]{3,2,1,0:T(8,128)(2,1)S(1)}, u32[]{:S(2)}, u32[]{:S(2)}) %all-to-all-start) | async-done | bytes 16416 | tf_op jit(solution)/shard_map/all_to_all | solution.py:31
  21.8 1.3 convolution_bitcast_fusion.7
  23.9 41.0 %psum.28 = bf16[4,2,8,128]{3,1,2,0:T(2,128)(2,1)S(1)} all-reduce(f32[4,2,8,128]{3,1,2,0:T(2,128)S(1)} %fusion.3), channel_id=1, replica_groups=mesh['group'=4,'member'=8] {'group','member'}, use_global_device_ids=true, to_apply=%region_0.0 | all-reduce | flops 8192 | bytes 49152 | tf_op jit(solution)/shard_map/psum | solution.py:85
  65.4 1.2 gather_fusion.3
  66.6 4.5 %all-to-all-start.1 = ((bf16[8,1,8,128]{3,2,1,0:T(8,128)(2,1)}), bf16[8,1,8,128]{3,2,1,0:T(8,128)(2,1)S(1)}, u32[]{:S(2)}, u32[]{:S(2)}) async-start(bf16[8,1,8,128]{3,2,1,0:T(8,128)(2,1)} %bitcast.21), calls=%async_computation.1 | async-start | bytes 32768 | tf_op jit(solution)/shard_map/all_to_all | solution.py:31
  71.6 1.3 collective-permute-start.2
  72.9 1.3 collective-permute-start.3
  74.3 3.6 %collective-permute-done.3 = bf16[1,4,8,128]{3,2,1,0:T(8,128)(2,1)S(1)} collective-permute-done((bf16[1,4,8,128]{3,2,1,0:T(8,128)(2,1)S(1)}, bf16[1,4,8,128]{3,2,1,0:T(8,128)(2,1)S(1)}, u32[]{:S(2)}, u32[]{:S(2)}) %collective-permute-start.3) | collective-permute-done | bytes 8224 | tf_op jit(solution)/shard_map/ppermute | solution.py:22
  78.6 0.6 copy-done.5
  79.5 1.2 gather_fusion.6
  81.2 4.3 %collective-permute-start.4 = (bf16[1,4,8,128]{3,2,1,0:T(8,128)(2,1)S(1)}, bf16[1,4,8,128]{3,2,1,0:T(8,128)(2,1)S(1)}, u32[]{:S(2)}, u32[]{:S(2)}) collective-permute-start(bf16[1,4,8,128]{3,2,1,0:T(8,128)(2,1)S(1)} %bitcast.147), channel_id=1, source_target_pairs={{0,8},{8,16},{16,24},{1,9},{9,17},{17,25},{2,10},{10,18},{18,26},{... | collective-permute-start | bytes 24584 | tf_op jit(solution)/shard_map/ppermute | solution.py:20
  85.5 1.3 collective-permute-start.5
  86.8 6.0 %all-to-all-start.2 = ((bf16[8,1,8,128]{3,2,1,0:T(8,128)(2,1)}), bf16[8,1,8,128]{3,2,1,0:T(8,128)(2,1)S(1)}, u32[]{:S(2)}, u32[]{:S(2)}) async-start(bf16[8,1,8,128]{3,2,1,0:T(8,128)(2,1)} %bitcast.30), calls=%async_computation.2 | async-start | bytes 32768 | tf_op jit(solution)/shard_map/all_to_all | solution.py:31
  93.0 6.5 %all-to-all-done.2 = bf16[8,1,8,128]{3,2,1,0:T(8,128)(2,1)S(1)} async-done(((bf16[8,1,8,128]{3,2,1,0:T(8,128)(2,1)}), bf16[8,1,8,128]{3,2,1,0:T(8,128)(2,1)S(1)}, u32[]{:S(2)}, u32[]{:S(2)}) %all-to-all-start.2) | async-done | bytes 16416 | tf_op jit(solution)/shard_map/all_to_all | solution.py:31
  100.6 39.3 %all-reduce = (f32[32,8]{0,1:T(8,128)S(1)}, f32[8,8]{0,1:T(8,128)S(1)}, f32[32,32]{1,0:T(8,128)S(1)}) all-reduce(f32[32,8]{0,1:T(8,128)S(1)} %fusion.15, f32[8,8]{0,1:T(8,128)S(1)} %fusion.13, f32[32,32]{1,0:T(8,128)S(1)} %fusion), channel_id=1, replica_groups=mesh['group'=4,'member'=8] {'group','member'}, use_global_device_ids=true, to_apply=%region_1.0 | all-reduce | flops 1344 | bytes 10752 | tf_op jit(solution)/shard_map/psum | solution.py:115
  141.3 0.7 cholesky.17
  142.7 0.6 fusion.20
  144.2 0.8 convolution_bitcast_fusion.1
  (68 shorter events, 9.0 us)
Async XLA Ops:
  0.6 64.3 %copy-start = (bf16[1024,256]{1,0:T(8,128)(2,1)S(1)}, bf16[1024,256]{1,0:T(8,128)(2,1)}, u32[]{:S(2)}) copy-start(bf16[1024,256]{1,0:T(8,128)(2,1)} %param.18) | copy-start | bytes 1572868
  2.9 3.7 %copy-start.10 = (s32[1,8,1]{1,2,0:T(1,128)S(1)}, s32[1,8,1]{1,2,0:T(1,128)}, u32[]{:S(2)}) copy-start(s32[1,8,1]{1,2,0:T(1,128)} %param.12) | copy-start | bytes 100
  2.9 11.8 %collective-permute-start = (bf16[1,4,8,128]{3,2,1,0:T(8,128)(2,1)S(1)}, bf16[1,4,8,128]{3,2,1,0:T(8,128)(2,1)S(1)}, u32[]{:S(2)}, u32[]{:S(2)}) collective-permute-start(bf16[1,4,8,128]{3,2,1,0:T(8,128)(2,1)S(1)} %bitcast.145), channel_id=1, source_target_pairs={{0,8},{8,16},{16,24},{1,9},{9,17},{17,25},{2,10},{10,18},{18,26},{... | collective-permute-start | bytes 24584 | tf_op jit(solution)/shard_map/ppermute | solution.py:20
  5.3 9.4 %collective-permute-start.1 = (bf16[1,4,8,128]{3,2,1,0:T(8,128)(2,1)S(1)}, bf16[1,4,8,128]{3,2,1,0:T(8,128)(2,1)S(1)}, u32[]{:S(2)}, u32[]{:S(2)}) collective-permute-start(bf16[1,4,8,128]{3,2,1,0:T(8,128)(2,1)S(1)} %bitcast.146), channel_id=1, source_target_pairs={{8,0},{16,8},{24,16},{9,1},{17,9},{25,17},{10,2},{18,10},{26,18},{... | collective-permute-start | bytes 24584 | tf_op jit(solution)/shard_map/ppermute | solution.py:22
  7.8 6.8 %copy-start.9 = (s32[2,8]{1,0:T(2,128)S(1)}, s32[2,8]{1,0:T(2,128)}, u32[]{:S(2)}) copy-start(s32[2,8]{1,0:T(2,128)} %param.11) | copy-start | bytes 196
  7.8 13.3 %all-to-all-start = ((bf16[8,1,8,128]{3,2,1,0:T(8,128)(2,1)}), bf16[8,1,8,128]{3,2,1,0:T(8,128)(2,1)S(1)}, u32[]{:S(2)}, u32[]{:S(2)}) async-start(bf16[8,1,8,128]{3,2,1,0:T(8,128)(2,1)} %bitcast.5), calls=%async_computation | async-start | bytes 32768 | tf_op jit(solution)/shard_map/all_to_all | solution.py:31
  21.8 1.3 copy-start.2
  21.8 1.3 copy-start.3
  21.8 1.3 copy-start.6
  23.1 0.7 copy-start.11
  23.3 55.1 %copy-start.1 = (bf16[2,8,128,128]{3,2,1,0:T(8,128)(2,1)S(1)}, bf16[2,8,128,128]{3,2,1,0:T(8,128)(2,1)}, u32[]{:S(2)}) copy-start(bf16[2,8,128,128]{3,2,1,0:T(8,128)(2,1)} %param.10) | copy-start | bytes 1572868
  66.6 11.2 %all-to-all-start.1 = ((bf16[8,1,8,128]{3,2,1,0:T(8,128)(2,1)}), bf16[8,1,8,128]{3,2,1,0:T(8,128)(2,1)S(1)}, u32[]{:S(2)}, u32[]{:S(2)}) async-start(bf16[8,1,8,128]{3,2,1,0:T(8,128)(2,1)} %bitcast.21), calls=%async_computation.1 | async-start | bytes 32768 | tf_op jit(solution)/shard_map/all_to_all | solution.py:31
  71.6 2.6 %collective-permute-start.2 = (bf16[1,4,8,128]{3,2,1,0:T(8,128)(2,1)S(1)}, bf16[1,4,8,128]{3,2,1,0:T(8,128)(2,1)S(1)}, u32[]{:S(2)}, u32[]{:S(2)}) collective-permute-start(bf16[1,4,8,128]{3,2,1,0:T(8,128)(2,1)S(1)} %bitcast.149), channel_id=1, source_target_pairs={{0,8},{8,16},{16,24},{1,9},{9,17},{17,25},{2,10},{10,18},{18,26},{... | collective-permute-start | bytes 24584 | tf_op jit(solution)/shard_map/ppermute | solution.py:20
  72.9 4.9 %collective-permute-start.3 = (bf16[1,4,8,128]{3,2,1,0:T(8,128)(2,1)S(1)}, bf16[1,4,8,128]{3,2,1,0:T(8,128)(2,1)S(1)}, u32[]{:S(2)}, u32[]{:S(2)}) collective-permute-start(bf16[1,4,8,128]{3,2,1,0:T(8,128)(2,1)S(1)} %bitcast.150), channel_id=1, source_target_pairs={{8,0},{16,8},{24,16},{9,1},{17,9},{25,17},{10,2},{18,10},{26,18},{... | collective-permute-start | bytes 24584 | tf_op jit(solution)/shard_map/ppermute | solution.py:22
  78.4 0.8 copy-start.5
  79.5 20.7 %copy-start.4 = (bf16[2,8,128]{2,1,0:T(8,128)(2,1)}, bf16[2,8,128]{2,1,0:T(8,128)(2,1)S(1)}, u32[]{:S(2)}) copy-start(bf16[2,8,128]{2,1,0:T(8,128)(2,1)S(1)} %fusion.9) | copy-start | bytes 12292
  81.2 11.7 %collective-permute-start.4 = (bf16[1,4,8,128]{3,2,1,0:T(8,128)(2,1)S(1)}, bf16[1,4,8,128]{3,2,1,0:T(8,128)(2,1)S(1)}, u32[]{:S(2)}, u32[]{:S(2)}) collective-permute-start(bf16[1,4,8,128]{3,2,1,0:T(8,128)(2,1)S(1)} %bitcast.147), channel_id=1, source_target_pairs={{0,8},{8,16},{16,24},{1,9},{9,17},{17,25},{2,10},{10,18},{18,26},{... | collective-permute-start | bytes 24584 | tf_op jit(solution)/shard_map/ppermute | solution.py:20
  85.5 7.4 %collective-permute-start.5 = (bf16[1,4,8,128]{3,2,1,0:T(8,128)(2,1)S(1)}, bf16[1,4,8,128]{3,2,1,0:T(8,128)(2,1)S(1)}, u32[]{:S(2)}, u32[]{:S(2)}) collective-permute-start(bf16[1,4,8,128]{3,2,1,0:T(8,128)(2,1)S(1)} %bitcast.148), channel_id=1, source_target_pairs={{8,0},{16,8},{24,16},{9,1},{17,9},{25,17},{10,2},{18,10},{26,18},{... | collective-permute-start | bytes 24584 | tf_op jit(solution)/shard_map/ppermute | solution.py:22
  86.8 12.6 %all-to-all-start.2 = ((bf16[8,1,8,128]{3,2,1,0:T(8,128)(2,1)}), bf16[8,1,8,128]{3,2,1,0:T(8,128)(2,1)S(1)}, u32[]{:S(2)}, u32[]{:S(2)}) async-start(bf16[8,1,8,128]{3,2,1,0:T(8,128)(2,1)} %bitcast.30), calls=%async_computation.2 | async-start | bytes 32768 | tf_op jit(solution)/shard_map/all_to_all | solution.py:31
  139.8 0.6 copy-start.7
  140.7 0.6 copy-start.8
where the time goes:
time: 146 us; the launch traced here: 145 us
  blocking collectives  80.2 us (55%)
  starting transfers between devices  29.1 us (20%)
  waiting for transfers between devices  16.5 us (11%)
  local copies, waits for them, and re-layouts  8.97 us (6%)
  matrix products  5.74 us (4%)
  other arithmetic  3.44 us (2%)
    psum x1, blocking collectives, local(): lax.psum(spread, ('group', 'member')).reshape(groups * CTG, NVEC, TILE)  41 us
    psum x1, blocking collectives, local(): lax.psum((coeff_part, self_part, basis_part), ('group', 'member'))  39.3 us
    all_to_all x3, starting transfers between devices, extend_tiles(): lax.all_to_all(outgoing, 'member', split_axis=0, concat_axis=0, tiled=True)  17.3 us
    all_to_all x3, waiting for transfers between devices, extend_tiles(): lax.all_to_all(outgoing, 'member', split_axis=0, concat_axis=0, tiled=True)  12.9 us
    ppermute x3, starting transfers between devices, extended_2(): lax.ppermute(tail, axis, [(i, (i + 1) % count) for i in range(ends)])  7.99 us
    ppermute x3, starting transfers between devices, extended_2(): lax.ppermute(head, axis, [((i + 1) % count, i) for i in range(ends)])  3.88 us
    ppermute x3, waiting for transfers between devices, extended_2(): lax.ppermute(head, axis, [((i + 1) % count, i) for i in range(ends)])  3.57 us
    gather x3, local copies, waits for them, and re-layouts, extend_tiles(): values[member_send[0].reshape(-1)].reshape(members, GH, NVEC, TILE)  3.5 us
  transfers between devices with their start and end apart: 9, of which 3 were waited for; matrix products, arithmetic and copies ran while one was open for 1% of the time, Pallas kernels for 0%

commit v1 on v0

v1 whole, which is shorter than its diff:
```python
import functools

import jax
import jax.numpy as jnp
from jax import lax
from jax.experimental import pallas as pl
from jax.experimental.pallas import tpu as pltpu
from jax.sharding import PartitionSpec as P

AXES = ("group", "member")
F32 = jnp.float32
BF16 = jnp.bfloat16
HIGH = lax.Precision.HIGHEST


def dot(left, right, contract=(1, 0), precision=None):
    return lax.dot_general(
        left,
        right,
        (((contract[0],), (contract[1],)), ((), ())),
        precision=precision,
        preferred_element_type=F32,
    )


def place():
    group, member = lax.axis_index("group"), lax.axis_index("member")
    return group, member, lax.axis_size("group"), lax.axis_size("member")


def fill_halo(send_ref, tiles_ref, member_send_ref):
    group, _, _, members = place()
    slots = member_send_ref.shape[2]
    count = tiles_ref.shape[0]
    everything = tiles_ref[...]
    send_ref[:, :count] = jnp.broadcast_to(everything[None], (send_ref.shape[0], *everything.shape))

    def one(peer, carry):
        for slot in range(slots):
            send_ref[group * members + peer, slot] = tiles_ref[member_send_ref[0, peer, slot]]
        return carry

    lax.fori_loop(0, members, one, 0, unroll=min(members, 8))


def fill_extended(ext_ref, own_ref, got_ref, table_ref, ghosts, rims):
    group, member, groups, members = place()
    count = own_ref.shape[0]
    ext_ref[:count] = own_ref[...]

    def one(peer, carry):
        for slot in range(ghosts):
            ext_ref[count + peer * ghosts + slot] = got_ref[group * members + peer, slot]
        return carry

    lax.fori_loop(0, members, one, 0, unroll=min(members, 8))
    base = count + members * ghosts
    for side in range(2):
        other = group - 1 if side == 0 else group + 1
        other = jnp.clip(other, 0, groups - 1)
        source = other * members + member
        tiles = [got_ref[source, j].astype(F32) for j in range(count)]
        for slot in range(rims):
            which = jnp.broadcast_to(table_ref[side, slot : slot + 1, :], tiles[0].shape)
            value = jnp.zeros_like(tiles[0])
            for j in range(count):
                value = jnp.where(which == j, tiles[j], value)
            ext_ref[base + side * rims + slot] = value.astype(BF16)


def apply_row(tile, ext_ref, own_ref, off_ref, cols_ref, diag_ref):
    total = dot(own_ref[tile], diag_ref[tile])
    for k in range(off_ref.shape[1]):
        total = total + dot(ext_ref[cols_ref[tile, k]], off_ref[tile, k])
    return total


def kernel_start(basis_ref, smoother_ref, member_send_ref, group_send_ref, first_ref, send_ref):
    count, vectors, width = first_ref.shape
    before = basis_ref.shape[1] - vectors
    for tile in range(count):
        first_ref[tile] = dot(basis_ref[tile, before:, :], smoother_ref[tile]).astype(BF16)
    fill_halo(send_ref, first_ref, member_send_ref)
    rows = lax.broadcasted_iota(jnp.int32, (vectors, width), 0)
    table = jnp.zeros((vectors, width), F32)
    for slot in range(group_send_ref.shape[1]):
        table = jnp.where(rows == slot, group_send_ref[0, slot].astype(F32), table)
    send_ref[:, count] = jnp.broadcast_to(table.astype(BF16)[None], (send_ref.shape[0], vectors, width))


def kernel_restrict(
    ghosts, rims, first_ref, got_ref, basis_ref, off_ref, cols_ref, diag_ref, prolong_ref, agg_ref,
    send_ref, table_ref, ext_ref,
):
    group, member, groups, members = place()
    count, vectors, _ = first_ref.shape
    before = basis_ref.shape[1] - vectors
    coarse = send_ref.shape[1]
    for side in range(2):
        other = group - 1 if side == 0 else group + 1
        inside = jnp.logical_and(other >= 0, other < groups)
        source = jnp.clip(other, 0, groups - 1) * members + member
        table = got_ref[source, count].astype(F32)
        table_ref[side] = jnp.where(inside, table, -1.0)
    fill_extended(ext_ref, first_ref, got_ref, table_ref, ghosts, rims)
    parts = [None] * coarse
    for tile in range(count):
        right = basis_ref[tile, before:, :].astype(F32)
        residual = (right - apply_row(tile, ext_ref, first_ref, off_ref, cols_ref, diag_ref)).astype(BF16)
        piece = dot(residual, prolong_ref[tile], (1, 1))
        for a in range(coarse):
            term = jnp.where(agg_ref[tile] == a, piece, 0.0)
            parts[a] = term if parts[a] is None else parts[a] + term
    for a in range(coarse):
        send_ref[:, a] = jnp.broadcast_to(parts[a].astype(BF16)[None], (send_ref.shape[0], *parts[a].shape))


def kernel_coarse(
    got_ref, inverse_ref, first_ref, prolong_ref, agg_ref, member_send_ref, second_ref, send_ref, fix_ref
):
    _, _, groups, members = place()
    count, vectors, width = first_ref.shape
    coarse = got_ref.shape[1]
    total = None
    for g in range(groups):
        for a in range(coarse):
            part = got_ref[g * members, a].astype(F32)
            for m in range(1, members):
                part = part + got_ref[g * members + m, a].astype(F32)
            start = (g * coarse + a) * width
            term = dot(part.astype(BF16), inverse_ref[start : start + width, :])
            total = term if total is None else total + term
    for a in range(coarse):
        fix_ref[a] = total[:, a * width : (a + 1) * width].astype(BF16)
    for tile in range(count):
        step = dot(fix_ref[agg_ref[tile]], prolong_ref[tile])
        second_ref[tile] = (first_ref[tile].astype(F32) + step).astype(BF16)
    fill_halo(send_ref, second_ref, member_send_ref)


def kernel_smooth(
    ghosts, rims, second_ref, got_ref, table_ref, basis_ref, off_ref, cols_ref, diag_ref, smoother_ref,
    member_send_ref, result_ref, send_ref, ext_ref,
):
    count, vectors, _ = second_ref.shape
    before = basis_ref.shape[1] - vectors
    fill_extended(ext_ref, second_ref, got_ref, table_ref, ghosts, rims)
    for tile in range(count):
        right = basis_ref[tile, before:, :].astype(F32)
        residual = (right - apply_row(tile, ext_ref, second_ref, off_ref, cols_ref, diag_ref)).astype(BF16)
        step = dot(residual, smoother_ref[tile])
        result_ref[tile] = (second_ref[tile].astype(F32) + step).astype(BF16)
    fill_halo(send_ref, result_ref, member_send_ref)


def pack_offsets(blocks):
    starts = []
    at = blocks + 1
    for i in range(blocks):
        starts.append(at)
        at += blocks - i
    return starts


def kernel_products(
    ghosts, rims, values_ref, got_ref, table_ref, basis_ref, off_ref, cols_ref, diag_ref,
    applied_ref, send_ref, ext_ref, wide_ref,
):
    count, vectors, width = values_ref.shape
    number = basis_ref.shape[1]
    blocks = number // vectors
    lanes = lax.broadcasted_iota(jnp.int32, (vectors, width), 1)
    fill_extended(ext_ref, values_ref, got_ref, table_ref, ghosts, rims)
    packed = None
    wide_ref[...] = jnp.zeros_like(wide_ref)
    for tile in range(count):
        applied = apply_row(tile, ext_ref, values_ref, off_ref, cols_ref, diag_ref).astype(BF16)
        applied_ref[tile] = applied
        wide_ref[:number] = basis_ref[tile].astype(F32)
        wide_ref[number : number + vectors] = applied.astype(F32)
        wide = wide_ref[...].astype(BF16)
        term = dot(applied, wide, (1, 1))
        for i, start in enumerate(pack_offsets(blocks)):
            own = dot(basis_ref[tile, i * vectors : (i + 1) * vectors, :], wide, (1, 1))
            moved = pltpu.roll(own, ((start - i) * vectors) % width, 1)
            inside = jnp.logical_and(lanes >= start * vectors, lanes < (start + blocks - i) * vectors)
            term = jnp.where(inside, moved, term)
        packed = term if packed is None else packed + term
    send_ref[...] = jnp.broadcast_to(packed[None], send_ref.shape)


def kernel_finish(scale, got_ref, applied_ref, basis_ref, coefficients_ref, gram_ref, block_ref, half_ref):
    count, vectors, width = applied_ref.shape
    number = basis_ref.shape[1]
    blocks = number // vectors
    total = jnp.sum(got_ref[...], axis=0) * scale
    turned = total[:, :number]
    own = total[:, number : number + vectors]
    coefficients_ref[...] = turned
    lanes = lax.broadcasted_iota(jnp.int32, (vectors, width), 1)
    rows = lax.broadcasted_iota(jnp.int32, (vectors, width), 0)
    for i, start in enumerate(pack_offsets(blocks)):
        moved = pltpu.roll(total, (i - start) * vectors % width, 1)
        first, last = i * vectors, (i + 1) * vectors
        inside = jnp.logical_and(lanes >= first, lanes < last)
        unit = jnp.where(lanes == rows + first, 1.0, 0.0)
        beyond = jnp.logical_and(lanes >= last, lanes < number)
        value = jnp.where(inside, unit - 0.5 * moved, jnp.where(beyond, -moved, 0.0))
        half_ref[i * vectors : (i + 1) * vectors, :] = value[:, :number]
    half = half_ref[...]
    weighted = dot(turned, half, (1, 1), HIGH)
    gram = own - dot(turned, weighted, (1, 1), HIGH) - dot(weighted, turned, (1, 1), HIGH)
    gram_ref[...] = gram
    square = lax.broadcasted_iota(jnp.int32, (vectors, vectors), 1)
    level = lax.broadcasted_iota(jnp.int32, (vectors, vectors), 0)
    left = gram
    right = jnp.where(square == level, 1.0, 0.0)
    for j in range(vectors):
        pivot = jnp.sqrt(left[j : j + 1, j : j + 1])
        line_left = left[j : j + 1, :] / pivot
        line_right = right[j : j + 1, :] / pivot
        factor = left[:, j : j + 1] / pivot
        below = level > j
        left = jnp.where(below, left - factor * line_left, left)
        right = jnp.where(below, right - factor * line_right, jnp.where(level == j, line_right, right))
    for tile in range(count):
        basis = basis_ref[tile].astype(F32)
        remainder = applied_ref[tile].astype(F32) - dot(turned, basis, (1, 0), HIGH)
        block_ref[tile] = dot(right, remainder, (1, 0), HIGH)


def spread(blocks):
    return lax.all_to_all(blocks, AXES, split_axis=0, concat_axis=0, tiled=True)


def local(
    off_tiles,
    off_cols,
    member_send,
    group_send,
    diag_tiles,
    smoother,
    agg_map,
    prolong,
    coarse_inv,
    krylov_basis,
):
    members = lax.axis_size("member")
    devices = lax.axis_size("group") * members
    count, width, _ = diag_tiles.shape
    number = krylov_basis.shape[1]
    ghosts, rims = member_send.shape[2], group_send.shape[1]
    coarse = coarse_inv.shape[1] // width
    extended = count + members * ghosts + 2 * rims
    vectors = 8
    tile = (vectors, width)
    halo = max(count, ghosts)
    vmem, smem = pl.BlockSpec(memory_space=pltpu.VMEM), pl.BlockSpec(memory_space=pltpu.SMEM)
    shape = jax.ShapeDtypeStruct
    ext = pltpu.VMEM((extended, *tile), BF16)

    def call(body, outs, ins, scratch=()):
        specs = [smem if a.dtype == jnp.int32 else vmem for a in ins]
        return pl.pallas_call(
            body,
            out_shape=tuple(outs),
            in_specs=specs,
            out_specs=tuple(vmem for _ in outs),
            scratch_shapes=scratch,
        )(*ins)

    own = shape((count, *tile), BF16)
    sent = shape((devices, halo, *tile), BF16)
    first, send = call(
        kernel_start,
        (own, shape((devices, halo + 1, *tile), BF16)),
        (krylov_basis, smoother, member_send, group_send),
    )
    send, table = call(
        functools.partial(kernel_restrict, ghosts, rims),
        (shape((devices, coarse, *tile), BF16), shape((2, *tile), F32)),
        (first, spread(send), krylov_basis, off_tiles, off_cols, diag_tiles, prolong, agg_map),
        (ext,),
    )
    second, send = call(
        kernel_coarse,
        (own, sent),
        (spread(send), coarse_inv, first, prolong, agg_map, member_send),
        (pltpu.VMEM((coarse, *tile), BF16),),
    )
    preconditioned, send = call(
        functools.partial(kernel_smooth, ghosts, rims),
        (own, sent),
        (second, spread(send), table, krylov_basis, off_tiles, off_cols, diag_tiles, smoother, member_send),
        (ext,),
    )
    applied, send = call(
        functools.partial(kernel_products, ghosts, rims),
        (own, shape((devices, *tile), F32)),
        (preconditioned, spread(send), table, krylov_basis, off_tiles, off_cols, diag_tiles),
        (ext, pltpu.VMEM((width, width), F32)),
    )
    turned, gram_matrix, new_block = call(
        functools.partial(kernel_finish, 1.0 / (count * width * devices)),
        (shape((vectors, number), F32), shape((vectors, vectors), F32), shape((count, *tile), F32)),
        (spread(send), applied, krylov_basis),
        (pltpu.VMEM((number, number), F32),),
    )
    return (preconditioned, turned.T, gram_matrix, new_block)


def solution(mesh):
    both = ("group", "member")
    placed = (
        P(both, None, None, None),
        P(both, None),
        P(both, None, None),
        P(both, None),
        P(both, None, None),
        P(both, None, None),
        P(both),
        P(both, None, None),
        P(None, "group"),
        P(both, None, None),
    )
    return jax.shard_map(
        local,
        mesh=mesh,
        in_specs=placed,
        out_specs=(P(both, None, None), P(), P(), P(both, None, None)),
        check_vma=False,
    )
```

time: 146 us -> 77 us (0.53)
  starting transfers between devices: 29.1 us -> 0 us
  blocking collectives: 80.2 us -> 60.1 us
  waiting for transfers between devices: 16.5 us -> 0 us
  Pallas kernels: 0 us -> 14.4 us
  local copies, waits for them, and re-layouts: 8.97 us -> 1.32 us
  matrix products: 5.74 us -> 0 us
  other arithmetic: 3.44 us -> 0 us
    psum x2 -> x0, blocking collectives: 80.2 us -> none  [the longest x1 41 us: local(): lax.psum(spread, ('group', 'member')).reshape(groups * CTG, NVEC, TILE)]
    all_to_all x0 -> x5, blocking collectives: none -> 60.1 us  [spread(): return lax.all_to_all(blocks, AXES, split_axis=0, concat_axis=0, tiled=True)]
    all_to_all x3 -> x0, starting transfers between devices: 17.3 us -> none  [extend_tiles(): lax.all_to_all(outgoing, 'member', split_axis=0, concat_axis=0, tiled=True)]
    pallas_call x0 -> x6, Pallas kernels: none -> 14.4 us  [call(): pl.pallas_call(body, out_shape=tuple(outs), in_specs=specs, out_specs=tup...]
    all_to_all x3 -> x0, waiting for transfers between devices: 12.9 us -> none  [extend_tiles(): lax.all_to_all(outgoing, 'member', split_axis=0, concat_axis=0, tiled=True)]
    ppermute x6 -> x0, starting transfers between devices: 11.9 us -> none  [the longest x3 7.99 us: extended_2(): lax.ppermute(tail, axis, [(i, (i + 1) % count) for i in range(ends)])]
    gather x9 -> x0, local copies, waits for them, and re-layouts: 6.91 us -> none  [the longest x3 3.5 us: extend_tiles(): values[member_send[0].reshape(-1)].reshape(members, GH, NVEC, TILE)]
    dot_general x19 -> x0, matrix products: 5.56 us -> none  [the longest x3 1.63 us: operate(): jnp.einsum('tkcj,tkji->tci', picked, off_tiles, preferred_element_type=jn...]
  transfers between devices with their start and end apart: 9 -> 0, of which waited for: 3 -> 0; matrix products, arithmetic and copies ran while one was open for 1% -> 0% of each run, Pallas kernels for 0% -> 0%
where the time goes in v1:
time: 77 us; the launch traced here: 76.4 us
  blocking collectives  60.1 us (78%)
  Pallas kernels  14.4 us (19%)
  local copies, waits for them, and re-layouts  1.32 us (2%)
    all_to_all x5, blocking collectives, spread(): return lax.all_to_all(blocks, AXES, split_axis=0, concat_axis=0, tiled=True)  60.1 us
    pallas_call x6, Pallas kernels, call(): pl.pallas_call(body, out_shape=tuple(outs), in_specs=specs, out_specs=tup...  14.4 us

profile of v1, /device:TPU:0, one launch (start us, length us, event | category | flops | bytes accessed | tf_op | source)
XLA Modules:
  0.0 76.4 jit_solution(15337908205679227236)
XLA Ops:
  0.6 1.3 %copy.14.member_send_ref = s32[1,8,1]{2,1,0:T(8,128)} copy(s32[1,8,1]{1,2,0:T(1,128)} %param.12) | data formatting | bytes 64 | tf_op args[2]
  2.0 1.7 %shard_map.129 = (bf16[2,8,128]{2,1,0:T(8,128)(2,1)}, bf16[32,3,8,128]{3,2,1,0:T(8,128)(2,1)}) custom-call(bf16[2,32,128]{2,1,0:T(8,128)(2,1)} %basis_ref.9, bf16[2,128,128]{2,1,0:T(8,128)(2,1)} %smoother_ref.3, s32[1,8,1]{2,1,0:T(8,128)} %copy.14.member_send_ref, s32[1,4]{1,0:T(1,128)} %group_send_ref.1), custom_call_target="tpu_custom_call" | custom-call | tf_op jit(solution)/shard_map/pallas_call | solution.py:264
  3.6 15.7 %all_to_all.25.got_ref = bf16[32,3,8,128]{3,2,1,0:T(8,128)(2,1)} all-to-all(bf16[32,3,8,128]{3,2,1,0:T(8,128)(2,1)} %get-tuple-element.18), channel_id=1, replica_groups=mesh['group'=4,'member'=8] {'group','member'}, dimensions={0} | all-to-all | bytes 393216 | tf_op jit(solution)/shard_map/all_to_all | solution.py:233
  19.4 2.5 %shard_map.130 = (bf16[32,2,8,128]{3,2,1,0:T(8,128)(2,1)}, f32[2,8,128]{2,1,0:T(8,128)}) custom-call(bf16[2,8,128]{2,1,0:T(8,128)(2,1)} %get-tuple-element.17.first_ref, bf16[32,3,8,128]{3,2,1,0:T(8,128)(2,1)} %all_to_all.25.got_ref, bf16[2,32,128]{2,1,0:T(8,128)(2,1)} %basis_ref.9, bf16[2,8,128,128]{3,2,1,0:T(8,128)(2,1)} %off_ref.5, s32[2,8]{1,0:T(2,128)} %cols_ref.5, ...), custom_call_target="tpu_custom_call" | custom-call | tf_op jit(solution)/shard_map/pallas_call | solution.py:264
  21.9 11.2 %all_to_all.26.got_ref = bf16[32,2,8,128]{3,2,1,0:T(8,128)(2,1)} all-to-all(bf16[32,2,8,128]{3,2,1,0:T(8,128)(2,1)} %get-tuple-element.19), channel_id=1, replica_groups=mesh['group'=4,'member'=8] {'group','member'}, dimensions={0} | all-to-all | bytes 262144 | tf_op jit(solution)/shard_map/all_to_all | solution.py:233
  33.1 2.1 %shard_map.131 = (bf16[2,8,128]{2,1,0:T(8,128)(2,1)}, bf16[32,2,8,128]{3,2,1,0:T(8,128)(2,1)}) custom-call(bf16[32,2,8,128]{3,2,1,0:T(8,128)(2,1)} %all_to_all.26.got_ref, bf16[1024,256]{1,0:T(8,128)(2,1)} %inverse_ref.1, bf16[2,8,128]{2,1,0:T(8,128)(2,1)} %get-tuple-element.17.first_ref, bf16[2,128,128]{2,1,0:T(8,128)(2,1)} %prolong_ref.3, s32[2]{0:T(128)} %agg_ref.3, ...), custom_call_target="tpu_custom_call" | custom-call | tf_op jit(solution)/shard_map/pallas_call | solution.py:264
  35.2 11.1 %all_to_all.27.got_ref = bf16[32,2,8,128]{3,2,1,0:T(8,128)(2,1)} all-to-all(bf16[32,2,8,128]{3,2,1,0:T(8,128)(2,1)} %get-tuple-element.21), channel_id=1, replica_groups=mesh['group'=4,'member'=8] {'group','member'}, dimensions={0} | all-to-all | bytes 262144 | tf_op jit(solution)/shard_map/all_to_all | solution.py:233
  46.2 2.5 %shard_map.132 = (bf16[2,8,128]{2,1,0:T(8,128)(2,1)}, bf16[32,2,8,128]{3,2,1,0:T(8,128)(2,1)}) custom-call(bf16[2,8,128]{2,1,0:T(8,128)(2,1)} %get-tuple-element.20.second_ref, bf16[32,2,8,128]{3,2,1,0:T(8,128)(2,1)} %all_to_all.27.got_ref, f32[2,8,128]{2,1,0:T(8,128)} %get-tuple-element.22.table_ref, bf16[2,32,128]{2,1,0:T(8,128)(2,1)} %basis_ref.9, ...), custom_call_target="tpu_custom_call" | custom-call | tf_op jit(solution)/shard_map/pallas_call | solution.py:264
  48.8 11.1 %all_to_all.28.got_ref = bf16[32,2,8,128]{3,2,1,0:T(8,128)(2,1)} all-to-all(bf16[32,2,8,128]{3,2,1,0:T(8,128)(2,1)} %get-tuple-element.24), channel_id=1, replica_groups=mesh['group'=4,'member'=8] {'group','member'}, dimensions={0} | all-to-all | bytes 262144 | tf_op jit(solution)/shard_map/all_to_all | solution.py:233
  59.8 2.7 %shard_map.133 = (bf16[2,8,128]{2,1,0:T(8,128)(2,1)}, f32[32,8,128]{2,1,0:T(8,128)}) custom-call(bf16[2,8,128]{2,1,0:T(8,128)(2,1)} %get-tuple-element.13.values_ref, bf16[32,2,8,128]{3,2,1,0:T(8,128)(2,1)} %all_to_all.28.got_ref, f32[2,8,128]{2,1,0:T(8,128)} %get-tuple-element.22.table_ref, bf16[2,32,128]{2,1,0:T(8,128)(2,1)} %basis_ref.9, ...), custom_call_target="tpu_custom_call" | custom-call | tf_op jit(solution)/shard_map/pallas_call | solution.py:264
  62.5 11.1 %all_to_all.29.got_ref = f32[32,8,128]{2,1,0:T(8,128)} all-to-all(f32[32,8,128]{2,1,0:T(8,128)} %get-tuple-element.25), channel_id=1, replica_groups=mesh['group'=4,'member'=8] {'group','member'}, dimensions={0} | all-to-all | bytes 262144 | tf_op jit(solution)/shard_map/all_to_all | solution.py:233
  73.6 2.9 %shard_map.134 = (f32[8,32]{1,0:T(8,128)}, f32[8,8]{1,0:T(8,128)}, f32[2,8,128]{2,1,0:T(8,128)}) custom-call(f32[32,8,128]{2,1,0:T(8,128)} %all_to_all.29.got_ref, bf16[2,8,128]{2,1,0:T(8,128)(2,1)} %get-tuple-element.26.applied_ref, bf16[2,32,128]{2,1,0:T(8,128)(2,1)} %basis_ref.9), custom_call_target="tpu_custom_call" | custom-call | tf_op jit(solution)/shard_map/pallas_call | solution.py:264

commit v2 on v1

v2 whole, which is shorter than its diff:
```python
import functools

import jax
import jax.numpy as jnp
from jax import lax
from jax.experimental import pallas as pl
from jax.experimental.pallas import tpu as pltpu
from jax.sharding import PartitionSpec as P

AXES = ("group", "member")
F32 = jnp.float32
BF16 = jnp.bfloat16
HIGH = lax.Precision.HIGHEST


def dot(left, right, contract=(1, 0), precision=None):
    return lax.dot_general(
        left,
        right,
        (((contract[0],), (contract[1],)), ((), ())),
        precision=precision,
        preferred_element_type=F32,
    )


def place():
    group, member = lax.axis_index("group"), lax.axis_index("member")
    return group, member, lax.axis_size("group"), lax.axis_size("member")


def fill_halo(send_ref, tiles, choice_ref):
    group, _, _, members = place()
    slots = choice_ref.shape[0] // members
    for j, tile in enumerate(tiles):
        narrow = tile.astype(BF16)
        send_ref[:, j] = jnp.broadcast_to(narrow[None], (send_ref.shape[0], *tile.shape))
    for slot in range(slots):
        for peer in range(members):
            value = pick(choice_ref[slot * members + peer], tiles)
            send_ref[group * members + peer, slot] = value.astype(BF16)


def pick(which, tiles):
    value = jnp.zeros_like(tiles[0])
    for j, tile in enumerate(tiles):
        value = jnp.where(which == j, tile, value)
    return value


def gather_rows(ext_ref, tiles, got_ref, rim_ref, select_ref, ghosts):
    group, member, groups, members = place()
    count, (vectors, width) = len(tiles), tiles[0].shape
    rims = rim_ref.shape[0] // 2
    extended = ext_ref.shape[0]
    narrow = [None] * extended
    for j, tile in enumerate(tiles):
        ext_ref[j] = tile
    for slot in range(ghosts):
        for peer in range(members):
            ext_ref[count + peer * ghosts + slot] = got_ref[group * members + peer, slot].astype(F32)
    base = count + members * ghosts
    for side in range(2):
        other = jnp.clip(group - 1 + 2 * side, 0, groups - 1) * members + member
        found = [got_ref[other, j].astype(F32) for j in range(count)]
        for slot in range(rims):
            at = side * rims + slot
            ext_ref[base + at] = pick(rim_ref[at], found)
    extended_rows = ext_ref[...].reshape(extended * vectors, width).astype(BF16)
    return dot(select_ref[...], extended_rows).astype(BF16)


def apply_rows(picked, tiles, off_ref, diag_ref):
    count, (vectors, width) = len(tiles), tiles[0].shape
    number = off_ref.shape[1]
    results = []
    for t in range(count):
        rows = [picked[(t * number + k) * vectors : (t * number + k + 1) * vectors] for k in range(number)]
        left = jnp.concatenate(rows, axis=1)
        right = off_ref[t].reshape(number * width, width)
        results.append(dot(tiles[t].astype(BF16), diag_ref[t]) + dot(left, right))
    return results


def kernel_start(
    off_hbm, cols_hbm, member_send_hbm, group_send_hbm, diag_hbm, smoother_hbm, agg_hbm, prolong_hbm, basis_hbm,
    first_ref, send_ref, choice_ref, select_ref, mine_ref, off_ref, diag_ref, smoother_ref, prolong_ref, basis_ref,
    cols_ref, member_send_ref, group_send_ref, agg_ref, sems,
):
    count, vectors, width = first_ref.shape
    pairs = (
        (basis_hbm, basis_ref),
        (smoother_hbm, smoother_ref),
        (member_send_hbm, member_send_ref),
        (group_send_hbm, group_send_ref),
        (cols_hbm, cols_ref),
        (agg_hbm, agg_ref),
        (off_hbm, off_ref),
        (diag_hbm, diag_ref),
        (prolong_hbm, prolong_ref),
    )
    copies = [pltpu.make_async_copy(a, b, sems.at[i]) for i, (a, b) in enumerate(pairs)]
    for copy in copies:
        copy.start()
    for copy in copies[:6]:
        copy.wait()
    before = basis_ref.shape[1] - vectors
    tiles = []
    for t in range(count):
        value = dot(basis_ref[t, before:, :], smoother_ref[t]).astype(BF16)
        first_ref[t] = value
        tiles.append(value.astype(F32))
    for at in range(member_send_ref.shape[1]):
        choice_ref[at] = jnp.full((vectors, width), member_send_ref[0, at].astype(F32))
    fill_halo(send_ref, tiles, choice_ref)
    rows = lax.broadcasted_iota(jnp.int32, (vectors, width), 0)
    table = jnp.zeros((vectors, width), F32)
    for slot in range(group_send_ref.shape[1]):
        table = jnp.where(rows == slot, group_send_ref[0, slot].astype(F32), table)
    send_ref[:, send_ref.shape[1] - 1] = jnp.broadcast_to(
        table.astype(BF16)[None], (send_ref.shape[0], vectors, width)
    )
    number = off_ref.shape[1]
    columns = select_ref.shape[1]
    ahead = lax.broadcasted_iota(jnp.int32, (vectors, columns), 1) - lax.broadcasted_iota(
        jnp.int32, (vectors, columns), 0
    )
    for t in range(count):
        blocks = [jnp.where(ahead == cols_ref[t, k] * vectors, 1.0, 0.0) for k in range(number)]
        select_ref[t * number * vectors : (t + 1) * number * vectors, :] = jnp.concatenate(blocks, 0).astype(BF16)
        mine_ref[t] = jnp.full((vectors, width), agg_ref[t].astype(F32))
    for copy in copies[6:]:
        copy.wait()


def kernel_restrict(
    ghosts, first_ref, got_ref, select_ref, mine_ref, off_ref, diag_ref, prolong_ref, basis_ref,
    send_ref, rim_ref, ext_ref,
):
    group, member, groups, members = place()
    count, vectors, width = first_ref.shape
    before = basis_ref.shape[1] - vectors
    coarse = send_ref.shape[1]
    rims = rim_ref.shape[0] // 2
    for side in range(2):
        other = group - 1 + 2 * side
        inside = jnp.logical_and(other >= 0, other < groups)
        source = jnp.clip(other, 0, groups - 1) * members + member
        table = got_ref[source, got_ref.shape[1] - 1].astype(F32)
        table = jnp.where(inside, table, -1.0)
        for slot in range(rims):
            rim_ref[side * rims + slot] = jnp.broadcast_to(table[slot : slot + 1, :], (vectors, width))
    tiles = [first_ref[t].astype(F32) for t in range(count)]
    picked = gather_rows(ext_ref, tiles, got_ref, rim_ref, select_ref, ghosts)
    products = apply_rows(picked, tiles, off_ref, diag_ref)
    parts = [jnp.zeros((vectors, width), F32) for _ in range(coarse)]
    for t in range(count):
        right = basis_ref[t, before:, :].astype(F32)
        piece = dot((right - products[t]).astype(BF16), prolong_ref[t], (1, 1))
        for a in range(coarse):
            parts[a] = parts[a] + jnp.where(mine_ref[t] == a, piece, 0.0)
    for a in range(coarse):
        send_ref[:, a] = jnp.broadcast_to(parts[a].astype(BF16)[None], (send_ref.shape[0], vectors, width))


def kernel_coarse(got_ref, inverse_ref, first_ref, choice_ref, mine_ref, prolong_ref, second_ref, send_ref):
    _, _, groups, members = place()
    count, vectors, width = first_ref.shape
    coarse = got_ref.shape[1]
    sums = []
    for g in range(groups):
        for a in range(coarse):
            part = got_ref[g * members, a].astype(F32)
            for m in range(1, members):
                part = part + got_ref[g * members + m, a].astype(F32)
            sums.append(part.astype(BF16))
    total = dot(jnp.concatenate(sums, axis=1), inverse_ref[...])
    fixes = [total[:, a * width : (a + 1) * width] for a in range(coarse)]
    tiles = []
    for t in range(count):
        step = dot(pick(mine_ref[t], fixes).astype(BF16), prolong_ref[t])
        value = (first_ref[t].astype(F32) + step).astype(BF16)
        second_ref[t] = value
        tiles.append(value.astype(F32))
    fill_halo(send_ref, tiles, choice_ref)


def kernel_smooth(
    ghosts, second_ref, got_ref, rim_ref, select_ref, choice_ref, off_ref, diag_ref, smoother_ref, basis_ref,
    result_ref, send_ref, ext_ref,
):
    count, vectors, _ = second_ref.shape
    before = basis_ref.shape[1] - vectors
    tiles = [second_ref[t].astype(F32) for t in range(count)]
    picked = gather_rows(ext_ref, tiles, got_ref, rim_ref, select_ref, ghosts)
    products = apply_rows(picked, tiles, off_ref, diag_ref)
    results = []
    for t in range(count):
        right = basis_ref[t, before:, :].astype(F32)
        step = dot((right - products[t]).astype(BF16), smoother_ref[t])
        value = (tiles[t] + step).astype(BF16)
        result_ref[t] = value
        results.append(value.astype(F32))
    fill_halo(send_ref, results, choice_ref)


def pack_offsets(blocks):
    starts = []
    at = blocks + 1
    for i in range(blocks):
        starts.append(at)
        at += blocks - i
    return starts


def kernel_products(
    ghosts, values_ref, got_ref, rim_ref, select_ref, off_ref, diag_ref, basis_ref,
    applied_ref, send_ref, values_hbm, ext_ref, sem,
):
    out = pltpu.make_async_copy(values_ref, values_hbm, sem)
    out.start()
    count, vectors, width = values_ref.shape
    number = basis_ref.shape[1]
    blocks = number // vectors
    lanes = lax.broadcasted_iota(jnp.int32, (vectors, width), 1)
    wides = []
    packed = [jnp.zeros((vectors, width), F32) for _ in range(blocks)]
    for t in range(count):
        basis = basis_ref[t]
        wide = jnp.concatenate([basis, jnp.zeros((width - number, width), BF16)], axis=0)
        wides.append(wide)
        whole = dot(basis, wide, (1, 1))
        for i in range(blocks):
            packed[i] = packed[i] + whole[i * vectors : (i + 1) * vectors, :]
    total = jnp.zeros((vectors, width), F32)
    for i, start in enumerate(pack_offsets(blocks)):
        moved = pltpu.roll(packed[i], ((start - i) * vectors) % width, 1)
        inside = jnp.logical_and(lanes >= start * vectors, lanes < (start + blocks - i) * vectors)
        total = jnp.where(inside, moved, total)
    tiles = [values_ref[t].astype(F32) for t in range(count)]
    picked = gather_rows(ext_ref, tiles, got_ref, rim_ref, select_ref, ghosts)
    products = apply_rows(picked, tiles, off_ref, diag_ref)
    own = jnp.zeros((vectors, width), F32)
    for t in range(count):
        applied = products[t].astype(BF16)
        applied_ref[t] = applied
        total = total + dot(applied, wides[t], (1, 1))
        tall = jnp.concatenate([applied.astype(F32), jnp.zeros((width - vectors, width), F32)], axis=0)
        own = own + dot(applied, tall.astype(BF16), (1, 1))
    total = total + pltpu.roll(own, number, 1)
    send_ref[...] = jnp.broadcast_to(total[None], send_ref.shape)
    out.wait()


def kernel_finish(scale, got_ref, applied_ref, basis_ref, coefficients_ref, gram_ref, block_ref, half_ref):
    count, vectors, width = applied_ref.shape
    number = basis_ref.shape[1]
    blocks = number // vectors
    total = jnp.sum(got_ref[...], axis=0) * scale
    turned = total[:, :number]
    own = total[:, number : number + vectors]
    coefficients_ref[...] = turned
    lanes = lax.broadcasted_iota(jnp.int32, (vectors, width), 1)
    rows = lax.broadcasted_iota(jnp.int32, (vectors, width), 0)
    for i, start in enumerate(pack_offsets(blocks)):
        moved = pltpu.roll(total, (i - start) * vectors % width, 1)
        first, last = i * vectors, (i + 1) * vectors
        inside = jnp.logical_and(lanes >= first, lanes < last)
        unit = jnp.where(lanes == rows + first, 1.0, 0.0)
        beyond = jnp.logical_and(lanes >= last, lanes < number)
        value = jnp.where(inside, unit - 0.5 * moved, jnp.where(beyond, -moved, 0.0))
        half_ref[i * vectors : (i + 1) * vectors, :] = value[:, :number]
    half = half_ref[...]
    weighted = dot(turned, half, (1, 1), HIGH)
    gram = own - dot(turned, weighted, (1, 1), HIGH) - dot(weighted, turned, (1, 1), HIGH)
    gram_ref[...] = gram
    square = lax.broadcasted_iota(jnp.int32, (vectors, vectors), 1)
    level = lax.broadcasted_iota(jnp.int32, (vectors, vectors), 0)
    left = gram
    right = jnp.where(square == level, 1.0, 0.0)
    for j in range(vectors):
        pivot = jnp.sqrt(left[j : j + 1, j : j + 1])
        line_left = left[j : j + 1, :] / pivot
        line_right = right[j : j + 1, :] / pivot
        factor = left[:, j : j + 1] / pivot
        below = level > j
        left = jnp.where(below, left - factor * line_left, left)
        right = jnp.where(below, right - factor * line_right, jnp.where(level == j, line_right, right))
    for tile in range(count):
        basis = basis_ref[tile].astype(F32)
        remainder = applied_ref[tile].astype(F32) - dot(turned, basis, (1, 0), HIGH)
        block_ref[tile] = dot(right, remainder, (1, 0), HIGH)


def spread(blocks):
    return lax.all_to_all(blocks, AXES, split_axis=0, concat_axis=0, tiled=True)


def local(
    off_tiles,
    off_cols,
    member_send,
    group_send,
    diag_tiles,
    smoother,
    agg_map,
    prolong,
    coarse_inv,
    krylov_basis,
):
    members = lax.axis_size("member")
    devices = lax.axis_size("group") * members
    count, width, _ = diag_tiles.shape
    number = krylov_basis.shape[1]
    ghosts, rims = member_send.shape[2], group_send.shape[1]
    coarse = coarse_inv.shape[1] // width
    extended = count + members * ghosts + 2 * rims
    vectors = 8
    tile = (vectors, width)
    halo = max(count, ghosts)
    k = off_tiles.shape[1]
    smem, hbm = pltpu.SMEM, pl.BlockSpec(memory_space=pltpu.HBM)
    vmem = pl.BlockSpec(memory_space=pltpu.VMEM)
    shape = jax.ShapeDtypeStruct
    ext = pltpu.VMEM((extended, *tile), F32)
    own = shape((count, *tile), BF16)
    sent = shape((devices, halo, *tile), BF16)

    def call(body, outs, ins, scratch=(), in_spec=vmem, in_hbm=()):
        return pl.pallas_call(
            body,
            out_shape=tuple(outs) + tuple(in_hbm),
            in_specs=[in_spec] * len(ins),
            out_specs=(vmem,) * len(outs) + (hbm,) * len(in_hbm),
            scratch_shapes=scratch,
            compiler_params=pltpu.CompilerParams(vmem_limit_bytes=8 * 1024 * 1024),
        )(*ins)

    peers = jnp.transpose(member_send, (0, 2, 1)).reshape(1, ghosts * members)
    outs = call(
        kernel_start,
        (
            own,
            shape((devices, halo + 1, *tile), BF16),
            shape((ghosts * members, *tile), F32),
            shape((count * k * vectors, extended * vectors), BF16),
            shape((count, *tile), F32),
            *(shape(a.shape, a.dtype) for a in (off_tiles, diag_tiles, smoother, prolong, krylov_basis)),
        ),
        [
            pltpu.with_memory_space_constraint(a, pltpu.HBM)
            for a in (off_tiles, off_cols, peers, group_send, diag_tiles, smoother, agg_map, prolong, krylov_basis)
        ],
        (
            smem(off_cols.shape, jnp.int32),
            smem(peers.shape, jnp.int32),
            smem(group_send.shape, jnp.int32),
            smem(agg_map.shape, jnp.int32),
            pltpu.SemaphoreType.DMA((9,)),
        ),
        hbm,
    )
    first, send, choice, select, mine, off, diag, smooth, prolonged, basis = outs
    send, rim = call(
        functools.partial(kernel_restrict, ghosts),
        (shape((devices, coarse, *tile), BF16), shape((2 * rims, *tile), F32)),
        (first, spread(send), select, mine, off, diag, prolonged, basis),
        (ext,),
    )
    second, send = call(
        kernel_coarse, (own, sent), (spread(send), coarse_inv, first, choice, mine, prolonged)
    )
    result, send = call(
        functools.partial(kernel_smooth, ghosts),
        (own, sent),
        (second, spread(send), rim, select, choice, off, diag, smooth, basis),
        (ext,),
    )
    applied, send, preconditioned = call(
        functools.partial(kernel_products, ghosts),
        (own, shape((devices, *tile), F32)),
        (result, spread(send), rim, select, off, diag, basis),
        (ext, pltpu.SemaphoreType.DMA),
        in_hbm=(own,),
    )
    turned, gram_matrix, new_block = call(
        functools.partial(kernel_finish, 1.0 / (count * width * devices)),
        (shape((vectors, number), F32), shape((vectors, vectors), F32), shape((count, *tile), F32)),
        (spread(send), applied, basis),
        (pltpu.VMEM((number, number), F32),),
    )
    return (preconditioned, turned.T, gram_matrix, new_block)


def solution(mesh):
    both = ("group", "member")
    placed = (
        P(both, None, None, None),
        P(both, None),
        P(both, None, None),
        P(both, None),
        P(both, None, None),
        P(both, None, None),
        P(both),
        P(both, None, None),
        P(None, "group"),
        P(both, None, None),
    )
    return jax.shard_map(
        local,
        mesh=mesh,
        in_specs=placed,
        out_specs=(P(both, None, None), P(), P(), P(both, None, None)),
        check_vma=False,
    )
```

time: 77 us -> 62.3 us (0.81)
  Pallas kernels: 14.4 us -> 5.08 us
  blocking collectives: 60.1 us -> 56.2 us
  local copies, waits for them, and re-layouts: 1.32 us -> 0.01 us
    pallas_call x6, Pallas kernels: 14.4 us -> 5.08 us  [call(): pl.pallas_call(body, out_shape=tuple(outs) + tuple(in_hbm), in_specs=[in_...]
    all_to_all x5, blocking collectives: 60.1 us -> 56.2 us  [spread(): return lax.all_to_all(blocks, AXES, split_axis=0, concat_axis=0, tiled=True)]
    unnamed x1 -> x2, local copies, waits for them, and re-layouts: 1.32 us -> 0.01 us
where the time goes in v2:
time: 62.3 us; the launch traced here: 62 us
  blocking collectives  56.2 us (90%)
  Pallas kernels  5.08 us (8%)
  between operations  0.68 us (1%)
    all_to_all x5, blocking collectives, spread(): return lax.all_to_all(blocks, AXES, split_axis=0, concat_axis=0, tiled=True)  56.2 us
    pallas_call x6, Pallas kernels, call(): pl.pallas_call(body, out_shape=tuple(outs) + tuple(in_hbm), in_specs=[in_...  5.08 us

profile of v2, /device:TPU:0, one launch (start us, length us, event | category | flops | bytes accessed | tf_op | source)
XLA Modules:
  0.0 62.0 jit_solution(16749823349736268649)
XLA Ops:
  0.6 1.2 %shard_map.129 = (bf16[2,8,128]{2,1,0:T(8,128)(2,1)S(1)}, bf16[32,3,8,128]{3,2,1,0:T(8,128)(2,1)S(1)}, f32[8,8,128]{2,1,0:T(8,128)S(1)}, bf16[128,144]{1,0:T(8,1...) custom-call(bf16[2,8,128,128]{3,2,1,0:T(8,128)(2,1)} %off_hbm.1, ...), custom_call_target="tpu_custom_call" | custom-call | tf_op jit(solution)/shard_map/pallas_call | solution.py:329
  1.8 15.4 %all_to_all.25.got_ref = bf16[32,3,8,128]{3,2,1,0:T(8,128)(2,1)S(1)} all-to-all(bf16[32,3,8,128]{3,2,1,0:T(8,128)(2,1)S(1)} %get-tuple-element.27), channel_id=1, replica_groups=mesh['group'=4,'member'=8] {'group','member'}, dimensions={0} | all-to-all | bytes 393216 | tf_op jit(solution)/shard_map/all_to_all | solution.py:295
  17.2 0.0 copy-start
  17.2 0.5 shard_map.130
  17.7 10.9 %all_to_all.26.got_ref = bf16[32,2,8,128]{3,2,1,0:T(8,128)(2,1)S(1)} all-to-all(bf16[32,2,8,128]{3,2,1,0:T(8,128)(2,1)S(1)} %get-tuple-element.34), channel_id=1, replica_groups=mesh['group'=4,'member'=8] {'group','member'}, dimensions={0} | all-to-all | bytes 262144 | tf_op jit(solution)/shard_map/all_to_all | solution.py:295
  28.6 0.0 copy-done
  28.6 0.4 shard_map.131
  29.0 10.0 %all_to_all.27.got_ref = bf16[32,2,8,128]{3,2,1,0:T(8,128)(2,1)S(1)} all-to-all(bf16[32,2,8,128]{3,2,1,0:T(8,128)(2,1)S(1)} %get-tuple-element.37), channel_id=1, replica_groups=mesh['group'=4,'member'=8] {'group','member'}, dimensions={0} | all-to-all | bytes 262144 | tf_op jit(solution)/shard_map/all_to_all | solution.py:295
  39.0 0.5 shard_map.132
  39.5 10.0 %all_to_all.28.got_ref = bf16[32,2,8,128]{3,2,1,0:T(8,128)(2,1)S(1)} all-to-all(bf16[32,2,8,128]{3,2,1,0:T(8,128)(2,1)S(1)} %get-tuple-element.41), channel_id=1, replica_groups=mesh['group'=4,'member'=8] {'group','member'}, dimensions={0} | all-to-all | bytes 262144 | tf_op jit(solution)/shard_map/all_to_all | solution.py:295
  49.4 0.6 shard_map.133
  50.1 10.0 %all_to_all.29.got_ref = f32[32,8,128]{2,1,0:T(8,128)S(1)} all-to-all(f32[32,8,128]{2,1,0:T(8,128)S(1)} %get-tuple-element.43), channel_id=1, replica_groups=mesh['group'=4,'member'=8] {'group','member'}, dimensions={0} | all-to-all | bytes 262144 | tf_op jit(solution)/shard_map/all_to_all | solution.py:295
  60.0 2.0 %shard_map.134 = (f32[8,32]{1,0:T(8,128)}, f32[8,8]{1,0:T(8,128)}, f32[2,8,128]{2,1,0:T(8,128)}) custom-call(f32[32,8,128]{2,1,0:T(8,128)S(1)} %all_to_all.29.got_ref, bf16[2,8,128]{2,1,0:T(8,128)(2,1)S(1)} %get-tuple-element.44.applied_ref, bf16[2,32,128]{2,1,0:T(8,128)(2,1)S(1)} %get-tuple-element.33.basis_ref), custom_call_target="tpu_custom_call" | custom-call | tf_op jit(solution)/shard_map/pallas_call | solution.py:329
Async XLA Ops:
  17.2 11.4 %copy-start = (bf16[1024,256]{1,0:T(8,128)(2,1)S(1)}, bf16[1024,256]{1,0:T(8,128)(2,1)}, u32[]{:S(2)}) copy-start(bf16[1024,256]{1,0:T(8,128)(2,1)} %inverse_ref.1) | copy-start | bytes 1572868

commit v3 on v2

--- a/solution.py
+++ b/solution.py
@@ -6,6 +6,7 @@
 from jax.experimental import pallas as pl
 from jax.experimental.pallas import tpu as pltpu
 from jax.sharding import PartitionSpec as P
+
 
 AXES = ("group", "member")
 F32 = jnp.float32
@@ -47,26 +48,35 @@
     return value
 
 
-def gather_rows(ext_ref, tiles, got_ref, rim_ref, select_ref, ghosts):
-    group, member, groups, members = place()
-    count, (vectors, width) = len(tiles), tiles[0].shape
-    rims = rim_ref.shape[0] // 2
-    extended = ext_ref.shape[0]
-    narrow = [None] * extended
+def select_rows(ext_ref, tiles, select_ref):
+    vectors, width = tiles[0].shape
     for j, tile in enumerate(tiles):
         ext_ref[j] = tile
-    for slot in range(ghosts):
-        for peer in range(members):
-            ext_ref[count + peer * ghosts + slot] = got_ref[group * members + peer, slot].astype(F32)
-    base = count + members * ghosts
-    for side in range(2):
-        other = jnp.clip(group - 1 + 2 * side, 0, groups - 1) * members + member
-        found = [got_ref[other, j].astype(F32) for j in range(count)]
-        for slot in range(rims):
-            at = side * rims + slot
-            ext_ref[base + at] = pick(rim_ref[at], found)
-    extended_rows = ext_ref[...].reshape(extended * vectors, width).astype(BF16)
-    return dot(select_ref[...], extended_rows).astype(BF16)
+    rows = ext_ref[...].reshape(ext_ref.shape[0] * vectors, width).astype(BF16)
+    return dot(select_ref[...], rows).astype(BF16)
+
+
+def place_rims(ext_ref, base, side, found, rim_ref):
+    rims = rim_ref.shape[0] // 2
+    for slot in range(rims):
+        at = side * rims + slot
+        ext_ref[base + at] = pick(rim_ref[at], found)
+
+
+def sides():
+    group, _, groups, _ = place()
+    odd = lax.rem(group, 2)
+    result = []
+    for side in (1 - odd, odd):
+        other = group - 1 + 2 * side
+        result.append((side, jnp.logical_and(other >= 0, other < groups)))
+    return result
+
+
+def tail_of(ref, count, vectors):
+    tail = ref[...].astype(F32)
+    parts = [tail[i * vectors : (i + 1) * vectors] for i in range(2 * count + 1)]
+    return parts[:count], parts[count], parts[count + 1 :]
 
 
 def apply_rows(picked, tiles, off_ref, diag_ref):
@@ -82,26 +92,23 @@
 
 
 def kernel_start(
-    off_hbm, cols_hbm, member_send_hbm, group_send_hbm, diag_hbm, smoother_hbm, agg_hbm, prolong_hbm, basis_hbm,
-    first_ref, send_ref, choice_ref, select_ref, mine_ref, off_ref, diag_ref, smoother_ref, prolong_ref, basis_ref,
-    cols_ref, member_send_ref, group_send_ref, agg_ref, sems,
+    smoother_hbm, prolong_hbm, basis_hbm, member_send_hbm, agg_hbm,
+    first_ref, parcel_ref, choice_ref, mine_ref, smoother_ref, prolong_ref, basis_ref,
+    member_send_ref, agg_ref, sems,
 ):
     count, vectors, width = first_ref.shape
+    members, ghosts = parcel_ref.shape[:2]
     pairs = (
         (basis_hbm, basis_ref),
         (smoother_hbm, smoother_ref),
         (member_send_hbm, member_send_ref),
-        (group_send_hbm, group_send_ref),
-        (cols_hbm, cols_ref),
         (agg_hbm, agg_ref),
-        (off_hbm, off_ref),
-        (diag_hbm, diag_ref),
         (prolong_hbm, prolong_ref),
     )
     copies = [pltpu.make_async_copy(a, b, sems.at[i]) for i, (a, b) in enumerate(pairs)]
     for copy in copies:
         copy.start()
-    for copy in copies[:6]:
+    for copy in copies:
         copy.wait()
     before = basis_ref.shape[1] - vectors
     tiles = []
@@ -109,48 +116,76 @@
         value = dot(basis_ref[t, before:, :], smoother_ref[t]).astype(BF16)
         first_ref[t] = value
         tiles.append(value.astype(F32))
-    for at in range(member_send_ref.shape[1]):
-        choice_ref[at] = jnp.full((vectors, width), member_send_ref[0, at].astype(F32))
-    fill_halo(send_ref, tiles, choice_ref)
+        mine_ref[t] = jnp.full((vectors, width), agg_ref[t].astype(F32))
+    for slot in range(ghosts):
+        for peer in range(members):
+            number = member_send_ref[0, slot * members + peer]
+            choice = jnp.full((vectors, width), number.astype(F32))
+            choice_ref[slot * members + peer] = choice
+            own = jnp.full((vectors, width), agg_ref[number].astype(F32))
+            parcel_ref[peer, slot, :width] = prolong_ref[number]
+            parcel_ref[peer, slot, width:] = jnp.concatenate([pick(choice, tiles), own], axis=0).astype(BF16)
+
+
+def kernel_stage(
+    off_hbm, diag_hbm, inverse_hbm, prolong_hbm, cols_hbm, group_send_hbm, first_ref, mine_ref,
+    swap_ref, head_ref, select_ref, off_ref, diag_ref,
+    cols_ref, group_send_ref, sems,
+):
+    count, vectors, width = first_ref.shape
+    long, columns = inverse_hbm.shape
+    coarse = columns // width
+    pairs = [(cols_hbm, cols_ref), (group_send_hbm, group_send_ref)]
+    for a in range(coarse):
+        pairs.append((inverse_hbm.at[:, a * width : (a + 1) * width], swap_ref.at[a * long : (a + 1) * long, :]))
+    at = coarse * long
+    for t in range(count):
+        pairs.append((prolong_hbm.at[t], swap_ref.at[at + t * width : at + (t + 1) * width, :]))
+    pairs += [(off_hbm, off_ref), (diag_hbm, diag_ref)]
+    copies = [pltpu.make_async_copy(a, b, sems.at[i]) for i, (a, b) in enumerate(pairs)]
+    for copy in copies:
+        copy.start()
+    for copy in copies[:2]:
+        copy.wait()
     rows = lax.broadcasted_iota(jnp.int32, (vectors, width), 0)
     table = jnp.zeros((vectors, width), F32)
     for slot in range(group_send_ref.shape[1]):
         table = jnp.where(rows == slot, group_send_ref[0, slot].astype(F32), table)
-    send_ref[:, send_ref.shape[1] - 1] = jnp.broadcast_to(
-        table.astype(BF16)[None], (send_ref.shape[0], vectors, width)
-    )
+    tail = [first_ref[t].astype(F32) for t in range(count)] + [table] + [mine_ref[t] for t in range(count)]
+    head_ref[...] = jnp.concatenate(tail + [jnp.zeros_like(table)], axis=0).astype(BF16)
     number = off_ref.shape[1]
-    columns = select_ref.shape[1]
-    ahead = lax.broadcasted_iota(jnp.int32, (vectors, columns), 1) - lax.broadcasted_iota(
-        jnp.int32, (vectors, columns), 0
+    wide = select_ref.shape[1]
+    ahead = lax.broadcasted_iota(jnp.int32, (vectors, wide), 1) - lax.broadcasted_iota(
+        jnp.int32, (vectors, wide), 0
     )
     for t in range(count):
         blocks = [jnp.where(ahead == cols_ref[t, k] * vectors, 1.0, 0.0) for k in range(number)]
         select_ref[t * number * vectors : (t + 1) * number * vectors, :] = jnp.concatenate(blocks, 0).astype(BF16)
-        mine_ref[t] = jnp.full((vectors, width), agg_ref[t].astype(F32))
-    for copy in copies[6:]:
+    for copy in copies[2:]:
         copy.wait()
 
 
 def kernel_restrict(
-    ghosts, first_ref, got_ref, select_ref, mine_ref, off_ref, diag_ref, prolong_ref, basis_ref,
+    first_ref, parcel_ref, even_ref, odd_ref, select_ref, mine_ref, off_ref, diag_ref, prolong_ref, basis_ref,
     send_ref, rim_ref, ext_ref,
 ):
-    group, member, groups, members = place()
     count, vectors, width = first_ref.shape
+    members, ghosts = parcel_ref.shape[:2]
     before = basis_ref.shape[1] - vectors
     coarse = send_ref.shape[1]
     rims = rim_ref.shape[0] // 2
-    for side in range(2):
-        other = group - 1 + 2 * side
-        inside = jnp.logical_and(other >= 0, other < groups)
-        source = jnp.clip(other, 0, groups - 1) * members + member
-        table = got_ref[source, got_ref.shape[1] - 1].astype(F32)
-        table = jnp.where(inside, table, -1.0)
+    base = count + members * ghosts
+    for ref, (side, exists) in zip((even_ref, odd_ref), sides(), strict=True):
+        found, table, _ = tail_of(ref, count, vectors)
+        table = jnp.where(exists, table, -1.0)
         for slot in range(rims):
             rim_ref[side * rims + slot] = jnp.broadcast_to(table[slot : slot + 1, :], (vectors, width))
+        place_rims(ext_ref, base, side, found, rim_ref)
     tiles = [first_ref[t].astype(F32) for t in range(count)]
-    picked = gather_rows(ext_ref, tiles, got_ref, rim_ref, select_ref, ghosts)
+    arrived = [
+        parcel_ref[peer, slot, width:].astype(F32)[:vectors] for peer in range(members) for slot in range(ghosts)
+    ]
+    picked = select_rows(ext_ref, tiles + arrived, select_ref)
     products = apply_rows(picked, tiles, off_ref, diag_ref)
     parts = [jnp.zeros((vectors, width), F32) for _ in range(coarse)]
     for t in range(count):
@@ -162,9 +197,22 @@
         send_ref[:, a] = jnp.broadcast_to(parts[a].astype(BF16)[None], (send_ref.shape[0], vectors, width))
 
 
-def kernel_coarse(got_ref, inverse_ref, first_ref, choice_ref, mine_ref, prolong_ref, second_ref, send_ref):
+def corrected(first, which, fixes, prolong):
+    return (first + dot(pick(which, fixes).astype(BF16), prolong)).astype(BF16).astype(F32)
+
+
+def fixes_of(sums, ref, coarse):
+    long = sums.shape[1]
+    return [dot(sums, ref[a * long : (a + 1) * long, :]) for a in range(coarse)]
+
+
+def kernel_sums(
+    got_ref, first_ref, parcel_ref, swap_ref, mine_ref, prolong_ref,
+    sums_ref, moved_ref,
+):
     _, _, groups, members = place()
-    count, vectors, width = first_ref.shape
+    count, _, width = first_ref.shape
+    ghosts = parcel_ref.shape[1]
     coarse = got_ref.shape[1]
     sums = []
     for g in range(groups):
@@ -173,25 +221,42 @@
             for m in range(1, members):
                 part = part + got_ref[g * members + m, a].astype(F32)
             sums.append(part.astype(BF16))
-    total = dot(jnp.concatenate(sums, axis=1), inverse_ref[...])
-    fixes = [total[:, a * width : (a + 1) * width] for a in range(coarse)]
-    tiles = []
-    for t in range(count):
-        step = dot(pick(mine_ref[t], fixes).astype(BF16), prolong_ref[t])
-        value = (first_ref[t].astype(F32) + step).astype(BF16)
-        second_ref[t] = value
-        tiles.append(value.astype(F32))
-    fill_halo(send_ref, tiles, choice_ref)
-
-
-def kernel_smooth(
-    ghosts, second_ref, got_ref, rim_ref, select_ref, choice_ref, off_ref, diag_ref, smoother_ref, basis_ref,
+    sums = jnp.concatenate(sums, axis=1)
+    sums_ref[...] = sums
+    fixes = fixes_of(sums, swap_ref, coarse)
+    for t in range(count):
+        moved_ref[t] = corrected(first_ref[t].astype(F32), mine_ref[t], fixes, prolong_ref[t])
+    for peer in range(members):
+        for slot in range(ghosts):
+            end = parcel_ref[peer, slot, width:].astype(F32)
+            vectors = end.shape[0] // 2
+            value = corrected(end[:vectors], end[vectors:], fixes, parcel_ref[peer, slot, :width])
+            moved_ref[count + peer * ghosts + slot] = value
+
+
+def kernel_cycle(
+    sums_ref, moved_ref, even_ref, odd_ref, even_head_ref, odd_head_ref, rim_ref, select_ref, choice_ref,
+    off_ref, diag_ref, smoother_ref, basis_ref,
     result_ref, send_ref, ext_ref,
 ):
-    count, vectors, _ = second_ref.shape
+    count, vectors, width = result_ref.shape
     before = basis_ref.shape[1] - vectors
-    tiles = [second_ref[t].astype(F32) for t in range(count)]
-    picked = gather_rows(ext_ref, tiles, got_ref, rim_ref, select_ref, ghosts)
+    sums = sums_ref[...]
+    at = even_ref.shape[0] - count * width
+    coarse = at // sums.shape[1]
+    base = moved_ref.shape[0]
+    swapped = ((even_ref, even_head_ref), (odd_ref, odd_head_ref))
+    for (ref, head_ref), (side, _) in zip(swapped, sides(), strict=True):
+        fixes = fixes_of(sums, ref, coarse)
+        found, _, theirs = tail_of(head_ref, count, vectors)
+        found = [
+            corrected(found[t], theirs[t], fixes, ref[at + t * width : at + (t + 1) * width, :])
+            for t in range(count)
+        ]
+        place_rims(ext_ref, base, side, found, rim_ref)
+    moved = [moved_ref[e] for e in range(base)]
+    tiles = moved[:count]
+    picked = select_rows(ext_ref, moved, select_ref)
     products = apply_rows(picked, tiles, off_ref, diag_ref)
     results = []
     for t in range(count):
@@ -237,7 +302,15 @@
         inside = jnp.logical_and(lanes >= start * vectors, lanes < (start + blocks - i) * vectors)
         total = jnp.where(inside, moved, total)
     tiles = [values_ref[t].astype(F32) for t in range(count)]
-    picked = gather_rows(ext_ref, tiles, got_ref, rim_ref, select_ref, ghosts)
+    group, member, groups, members = place()
+    arrived = [
+        got_ref[group * members + peer, slot].astype(F32) for peer in range(members) for slot in range(ghosts)
+    ]
+    for side in range(2):
+        other = jnp.clip(group - 1 + 2 * side, 0, groups - 1) * members + member
+        found = [got_ref[other, j].astype(F32) for j in range(count)]
+        place_rims(ext_ref, count + len(arrived), side, found, rim_ref)
+    picked = select_rows(ext_ref, tiles + arrived, select_ref)
     products = apply_rows(picked, tiles, off_ref, diag_ref)
     own = jnp.zeros((vectors, width), F32)
     for t in range(count):
@@ -325,54 +398,75 @@
     own = shape((count, *tile), BF16)
     sent = shape((devices, halo, *tile), BF16)
 
-    def call(body, outs, ins, scratch=(), in_spec=vmem, in_hbm=()):
+    def call(body, outs, ins, scratch=(), in_specs=None, in_hbm=()):
         return pl.pallas_call(
             body,
             out_shape=tuple(outs) + tuple(in_hbm),
-            in_specs=[in_spec] * len(ins),
+            in_specs=in_specs or [vmem] * len(ins),
             out_specs=(vmem,) * len(outs) + (hbm,) * len(in_hbm),
             scratch_shapes=scratch,
             compiler_params=pltpu.CompilerParams(vmem_limit_bytes=8 * 1024 * 1024),
         )(*ins)
 
+    def stay(*arrays):
+        return [pltpu.with_memory_space_constraint(a, pltpu.HBM) for a in arrays]
+
+    groups = devices // members
     peers = jnp.transpose(member_send, (0, 2, 1)).reshape(1, ghosts * members)
-    outs = call(
+    first, parcel, choice, mine, smooth, prolonged, basis = call(
         kernel_start,
         (
             own,
-            shape((devices, halo + 1, *tile), BF16),
+            shape((members, ghosts, width + 2 * vectors, width), BF16),
             shape((ghosts * members, *tile), F32),
+            shape((count, *tile), F32),
+            *(shape(a.shape, a.dtype) for a in (smoother, prolong, krylov_basis)),
+        ),
+        stay(smoother, prolong, krylov_basis, peers, agg_map),
+        (smem(peers.shape, jnp.int32), smem(agg_map.shape, jnp.int32), pltpu.SemaphoreType.DMA((5,))),
+        [hbm] * 5,
+    )
+    rows = coarse * coarse_inv.shape[0] + count * width
+    swap, head, select, off, diag = call(
+        kernel_stage,
+        (
+            shape((rows, width), BF16),
+            shape((vectors * (2 * count + 2), width), BF16),
             shape((count * k * vectors, extended * vectors), BF16),
-            shape((count, *tile), F32),
-            *(shape(a.shape, a.dtype) for a in (off_tiles, diag_tiles, smoother, prolong, krylov_basis)),
+            *(shape(a.shape, a.dtype) for a in (off_tiles, diag_tiles)),
         ),
-        [
-            pltpu.with_memory_space_constraint(a, pltpu.HBM)
-            for a in (off_tiles, off_cols, peers, group_send, diag_tiles, smoother, agg_map, prolong, krylov_basis)
-        ],
+        [*stay(off_tiles, diag_tiles, coarse_inv, prolong, off_cols, group_send), first, mine],
         (
             smem(off_cols.shape, jnp.int32),
-            smem(peers.shape, jnp.int32),
             smem(group_send.shape, jnp.int32),
-            smem(agg_map.shape, jnp.int32),
-            pltpu.SemaphoreType.DMA((9,)),
+            pltpu.SemaphoreType.DMA((4 + coarse + count,)),
         ),
-        hbm,
-    )
-    first, send, choice, select, mine, off, diag, smooth, prolonged, basis = outs
+        [hbm] * 6 + [vmem] * 2,
+    )
+    parcel = lax.all_to_all(parcel, "member", split_axis=0, concat_axis=0, tiled=True)
+    pairs = [
+        [(i + a, i + 1 - a) for i in range(start, groups - 1, 2) for a in (0, 1)] for start in (0, 1)
+    ]
+    even_head, odd_head = (lax.ppermute(head, "group", p) for p in pairs)
+    even, odd = (lax.ppermute(swap, "group", p) for p in pairs)
     send, rim = call(
-        functools.partial(kernel_restrict, ghosts),
+        kernel_restrict,
         (shape((devices, coarse, *tile), BF16), shape((2 * rims, *tile), F32)),
-        (first, spread(send), select, mine, off, diag, prolonged, basis),
+        (first, parcel, even_head, odd_head, select, mine, off, diag, prolonged, basis),
         (ext,),
     )
-    second, send = call(
-        kernel_coarse, (own, sent), (spread(send), coarse_inv, first, choice, mine, prolonged)
+    sums, moved = call(
+        kernel_sums,
+        (shape((vectors, coarse_inv.shape[0]), BF16), shape((count + ghosts * members, *tile), F32)),
+        (spread(send), first, parcel, swap, mine, prolonged),
     )
     result, send = call(
-        functools.partial(kernel_smooth, ghosts),
+        kernel_cycle,
         (own, sent),
-        (second, spread(send), rim, select, choice, off, diag, smooth, basis),
+        (
+            sums, moved, even, odd, even_head, odd_head, rim, select, choice,
+            off, diag, smooth, basis,
+        ),
         (ext,),
     )
     applied, send, preconditioned = call(
@@ -405,6 +499,7 @@
         P(None, "group"),
         P(both, None, None),
     )
+
     return jax.shard_map(
         local,
         mesh=mesh,

time: 62.3 us -> 60.8 us (0.976)
  blocking collectives: 56.2 us -> 36.6 us
  starting transfers between devices: 0 us -> 12.9 us
  waiting for transfers between devices: 0 us -> 2.68 us
  Pallas kernels: 5.08 us -> 7.49 us
    all_to_all x5 -> x3, blocking collectives: 56.2 us -> 36.6 us  [spread(): return lax.all_to_all(blocks, AXES, split_axis=0, concat_axis=0, tiled=True)]
    all_to_all x0 -> x1, starting transfers between devices: none -> 7.29 us  [local(): lax.all_to_all(parcel, 'member', split_axis=0, concat_axis=0, tiled=True)]
    ppermute x0 -> x4, starting transfers between devices: none -> 5.61 us  [the longest x2 3.61 us: local(): even, odd = (lax.ppermute(swap, 'group', p) for p in pairs)]
    pallas_call x6 -> x7, Pallas kernels: 5.08 us -> 7.49 us  [call(): pl.pallas_call(body, out_shape=tuple(outs) + tuple(in_hbm), in_specs=in_s...]
    all_to_all x0 -> x1, waiting for transfers between devices: none -> 1.84 us  [local(): lax.all_to_all(parcel, 'member', split_axis=0, concat_axis=0, tiled=True)]
    ppermute x0 -> x4, waiting for transfers between devices: none -> 0.84 us  [the longest x2 0.83 us: local(): even_head, odd_head = (lax.ppermute(head, 'group', p) for p in pairs)]
  transfers between devices with their start and end apart: 0 -> 5, of which waited for: 0 -> 2; matrix products, arithmetic and copies ran while one was open for 0% -> 0% of each run, Pallas kernels for 0% -> 4%
where the time goes in v3:
time: 60.8 us; the launch traced here: 60.4 us
  blocking collectives  36.6 us (60%)
  starting transfers between devices  12.9 us (21%)
  Pallas kernels  7.49 us (12%)
  waiting for transfers between devices  2.68 us (4%)
  between operations  0.7 us (1%)
    all_to_all x3, blocking collectives, spread(): return lax.all_to_all(blocks, AXES, split_axis=0, concat_axis=0, tiled=True)  36.6 us
    pallas_call x7, Pallas kernels, call(): pl.pallas_call(body, out_shape=tuple(outs) + tuple(in_hbm), in_specs=in_s...  7.49 us
    all_to_all x1, starting transfers between devices, local(): lax.all_to_all(parcel, 'member', split_axis=0, concat_axis=0, tiled=True)  7.29 us
    ppermute x2, starting transfers between devices, local(): even, odd = (lax.ppermute(swap, 'group', p) for p in pairs)  3.61 us
    ppermute x2, starting transfers between devices, local(): even_head, odd_head = (lax.ppermute(head, 'group', p) for p in pairs)  2 us
    all_to_all x1, waiting for transfers between devices, local(): lax.all_to_all(parcel, 'member', split_axis=0, concat_axis=0, tiled=True)  1.84 us
  transfers between devices with their start and end apart: 5, of which 2 were waited for; matrix products, arithmetic and copies ran while one was open for 0% of the time, Pallas kernels for 4%

profile of v3, /device:TPU:0, one launch (start us, length us, event | category | flops | bytes accessed | tf_op | source)
XLA Modules:
  0.0 60.4 jit_solution(12208334191227309653)
XLA Ops:
  0.6 1.8 %shard_map.129 = (bf16[2,8,128]{2,1,0:T(8,128)(2,1)S(1)}, bf16[8,1,144,128]{3,2,1,0:T(8,128)(2,1)}, f32[8,8,128]{2,1,0:T(8,128)S(1)}, f32[2,8,128]{2,1,0:T(8,128...) custom-call(bf16[2,128,128]{2,1,0:T(8,128)(2,1)} %smoother_hbm.1, ...), custom_call_target="tpu_custom_call" | custom-call | tf_op jit(solution)/shard_map/pallas_call | solution.py:402
  2.4 7.3 %all-to-all-start = ((bf16[8,1,144,128]{3,2,1,0:T(8,128)(2,1)}), bf16[8,1,144,128]{3,2,1,0:T(8,128)(2,1)S(1)}, u32[]{:S(2)}, u32[]{:S(2)}) async-start(bf16[8,1,144,128]{3,2,1,0:T(8,128)(2,1)} %get-tuple-element.29), calls=%async_computation | async-start | bytes 589824 | tf_op jit(solution)/shard_map/all_to_all | solution.py:446
  9.7 1.3 %shard_map.130 = (bf16[2304,128]{1,0:T(8,128)(2,1)S(1)}, bf16[48,128]{1,0:T(8,128)(2,1)S(1)}, bf16[128,144]{1,0:T(8,128)(2,1)S(1)}, bf16[2,8,128,128]{3,2,1,0:T(8,128)(2,1)S(1)}, bf16[2,128,128]{2,1,0:T(8,128)(2,1)S(1)}) custom-call(bf16[2,8,128,128]{3,2,1,0:T(8,128)(2,1)} %off_hbm.1, bf16[2,128,128]{2,1,0:T(8,128)(2,1)} %diag_hbm.1, ...), custom_call_target="tpu_custom_call" | custom-call | tf_op jit(solution)/shard_map/pallas_call | solution.py:402
  11.0 0.7 %collective-permute-start.3 = (bf16[2304,128]{1,0:T(8,128)(2,1)S(1)}, bf16[2304,128]{1,0:T(8,128)(2,1)S(1)}, u32[]{:S(2)}, u32[]{:S(2)}) collective-permute-start(bf16[2304,128]{1,0:T(8,128)(2,1)S(1)} %get-tuple-element.38.swap_ref), channel_id=1, source_target_pairs={{8,16},{16,8},{9,17},{17,9},{10,18},{18,10},{11,19},{19,11},{12,20... | collective-permute-start | bytes 1769480 | tf_op jit(solution)/shard_map/ppermute | solution.py:451
  11.7 2.9 %collective-permute-start.2 = (bf16[2304,128]{1,0:T(8,128)(2,1)S(1)}, bf16[2304,128]{1,0:T(8,128)(2,1)S(1)}, u32[]{:S(2)}, u32[]{:S(2)}) collective-permute-start(bf16[2304,128]{1,0:T(8,128)(2,1)S(1)} %get-tuple-element.38.swap_ref), channel_id=1, source_target_pairs={{0,8},{8,0},{16,24},{24,16},{1,9},{9,1},{17,25},{25,17},{2,10},{10... | collective-permute-start | bytes 1769480 | tf_op jit(solution)/shard_map/ppermute | solution.py:451
  14.7 0.7 %collective-permute-start.1 = (bf16[48,128]{1,0:T(8,128)(2,1)S(1)}, bf16[48,128]{1,0:T(8,128)(2,1)S(1)}, u32[]{:S(2)}, u32[]{:S(2)}) collective-permute-start(bf16[48,128]{1,0:T(8,128)(2,1)S(1)} %get-tuple-element.31), channel_id=1, source_target_pairs={{8,16},{16,8},{9,17},{17,9},{10,18},{18,10},{11,19},{19,11},{12,20... | collective-permute-start | bytes 36872 | tf_op jit(solution)/shard_map/ppermute | solution.py:450
  15.3 1.3 %collective-permute-start = (bf16[48,128]{1,0:T(8,128)(2,1)S(1)}, bf16[48,128]{1,0:T(8,128)(2,1)S(1)}, u32[]{:S(2)}, u32[]{:S(2)}) collective-permute-start(bf16[48,128]{1,0:T(8,128)(2,1)S(1)} %get-tuple-element.31), channel_id=1, source_target_pairs={{0,8},{8,0},{16,24},{24,16},{1,9},{9,1},{17,25},{25,17},{2,10},{10... | collective-permute-start | bytes 36872 | tf_op jit(solution)/shard_map/ppermute | solution.py:450
  16.7 0.0 collective-permute-done.1.odd_ref.odd_head_ref
  16.7 0.8 %collective-permute-done.even_ref.even_head_ref = bf16[48,128]{1,0:T(8,128)(2,1)S(1)} collective-permute-done((bf16[48,128]{1,0:T(8,128)(2,1)S(1)}, bf16[48,128]{1,0:T(8,128)(2,1)S(1)}, u32[]{:S(2)}, u32[]{:S(2)}) %collective-permute-start) | collective-permute-done | bytes 12320 | tf_op jit(solution)/shard_map/ppermute | solution.py:450
  17.5 1.8 %all-to-all-done.parcel_ref = bf16[8,1,144,128]{3,2,1,0:T(8,128)(2,1)S(1)} async-done(((bf16[8,1,144,128]{3,2,1,0:T(8,128)(2,1)}), bf16[8,1,144,128]{3,2,1,0:T(8,128)(2,1)S(1)}, u32[]{:S(2)}, u32[]{:S(2)}) %all-to-all-start) | async-done | bytes 294944 | tf_op jit(solution)/shard_map/all_to_all | solution.py:446
  19.3 0.5 shard_map.131
  19.8 16.7 %all_to_all.20.got_ref = bf16[32,2,8,128]{3,2,1,0:T(8,128)(2,1)S(1)} all-to-all(bf16[32,2,8,128]{3,2,1,0:T(8,128)(2,1)S(1)} %get-tuple-element.37), channel_id=1, replica_groups=mesh['group'=4,'member'=8] {'group','member'}, dimensions={0} | all-to-all | bytes 262144 | tf_op jit(solution)/shard_map/all_to_all | solution.py:368
  36.5 0.4 shard_map.132
  36.9 0.0 collective-permute-done.3.odd_ref
  36.9 0.0 collective-permute-done.2.even_ref
  36.9 1.0 %shard_map.133 = (bf16[2,8,128]{2,1,0:T(8,128)(2,1)S(1)}, bf16[32,2,8,128]{3,2,1,0:T(8,128)(2,1)S(1)}) custom-call(bf16[8,1024]{1,0:T(8,128)(2,1)S(1)} %get-tuple-element.39.sums_ref, f32[10,8,128]{2,1,0:T(8,128)S(1)} %get-tuple-element.40.moved_ref, bf16[2304,128]{1,0:T(8,128)(2,1)S(1)} %collective-permute-done.2.even_ref, ...), custom_call_target="tpu_custom_call" | custom-call | tf_op jit(solution)/shard_map/pallas_call | solution.py:402
  37.9 10.0 %all_to_all.21.got_ref = bf16[32,2,8,128]{3,2,1,0:T(8,128)(2,1)S(1)} all-to-all(bf16[32,2,8,128]{3,2,1,0:T(8,128)(2,1)S(1)} %get-tuple-element.45), channel_id=1, replica_groups=mesh['group'=4,'member'=8] {'group','member'}, dimensions={0} | all-to-all | bytes 262144 | tf_op jit(solution)/shard_map/all_to_all | solution.py:368
  47.9 0.6 %shard_map.134 = (bf16[2,8,128]{2,1,0:T(8,128)(2,1)S(1)}, f32[32,8,128]{2,1,0:T(8,128)S(1)}, bf16[2,8,128]{2,1,0:T(8,128)(2,1)}) custom-call(bf16[2,8,128]{2,1,0:T(8,128)(2,1)S(1)} %get-tuple-element.44.values_ref, bf16[32,2,8,128]{3,2,1,0:T(8,128)(2,1)S(1)} %all_to_all.21.got_ref, f32[8,8,128]{2,1,0:T(8,128)S(1)} %get-tuple-element.41.rim_ref, ...), custom_call_target="tpu_custom_call" | custom-call | tf_op jit(solution)/shard_map/pallas_call | solution.py:402
  48.5 10.0 %all_to_all.22.got_ref = f32[32,8,128]{2,1,0:T(8,128)S(1)} all-to-all(f32[32,8,128]{2,1,0:T(8,128)S(1)} %get-tuple-element.47), channel_id=1, replica_groups=mesh['group'=4,'member'=8] {'group','member'}, dimensions={0} | all-to-all | bytes 262144 | tf_op jit(solution)/shard_map/all_to_all | solution.py:368
  58.5 2.0 %shard_map.135 = (f32[8,32]{1,0:T(8,128)}, f32[8,8]{1,0:T(8,128)}, f32[2,8,128]{2,1,0:T(8,128)}) custom-call(f32[32,8,128]{2,1,0:T(8,128)S(1)} %all_to_all.22.got_ref, bf16[2,8,128]{2,1,0:T(8,128)(2,1)S(1)} %get-tuple-element.48.applied_ref, bf16[2,32,128]{2,1,0:T(8,128)(2,1)S(1)} %get-tuple-element.36.basis_ref), custom_call_target="tpu_custom_call" | custom-call | tf_op jit(solution)/shard_map/pallas_call | solution.py:402
Async XLA Ops:
  2.4 16.9 %all-to-all-start = ((bf16[8,1,144,128]{3,2,1,0:T(8,128)(2,1)}), bf16[8,1,144,128]{3,2,1,0:T(8,128)(2,1)S(1)}, u32[]{:S(2)}, u32[]{:S(2)}) async-start(bf16[8,1,144,128]{3,2,1,0:T(8,128)(2,1)} %get-tuple-element.29), calls=%async_computation | async-start | bytes 589824 | tf_op jit(solution)/shard_map/all_to_all | solution.py:446
  11.0 25.9 %collective-permute-start.3 = (bf16[2304,128]{1,0:T(8,128)(2,1)S(1)}, bf16[2304,128]{1,0:T(8,128)(2,1)S(1)}, u32[]{:S(2)}, u32[]{:S(2)}) collective-permute-start(bf16[2304,128]{1,0:T(8,128)(2,1)S(1)} %get-tuple-element.38.swap_ref), channel_id=1, source_target_pairs={{8,16},{16,8},{9,17},{17,9},{10,18},{18,10},{11,19},{19,11},{12,20... | collective-permute-start | bytes 1769480 | tf_op jit(solution)/shard_map/ppermute | solution.py:451
  11.7 25.2 %collective-permute-start.2 = (bf16[2304,128]{1,0:T(8,128)(2,1)S(1)}, bf16[2304,128]{1,0:T(8,128)(2,1)S(1)}, u32[]{:S(2)}, u32[]{:S(2)}) collective-permute-start(bf16[2304,128]{1,0:T(8,128)(2,1)S(1)} %get-tuple-element.38.swap_ref), channel_id=1, source_target_pairs={{0,8},{8,0},{16,24},{24,16},{1,9},{9,1},{17,25},{25,17},{2,10},{10... | collective-permute-start | bytes 1769480 | tf_op jit(solution)/shard_map/ppermute | solution.py:451
  14.7 2.0 %collective-permute-start.1 = (bf16[48,128]{1,0:T(8,128)(2,1)S(1)}, bf16[48,128]{1,0:T(8,128)(2,1)S(1)}, u32[]{:S(2)}, u32[]{:S(2)}) collective-permute-start(bf16[48,128]{1,0:T(8,128)(2,1)S(1)} %get-tuple-element.31), channel_id=1, source_target_pairs={{8,16},{16,8},{9,17},{17,9},{10,18},{18,10},{11,19},{19,11},{12,20... | collective-permute-start | bytes 36872 | tf_op jit(solution)/shard_map/ppermute | solution.py:450
  15.3 2.2 %collective-permute-start = (bf16[48,128]{1,0:T(8,128)(2,1)S(1)}, bf16[48,128]{1,0:T(8,128)(2,1)S(1)}, u32[]{:S(2)}, u32[]{:S(2)}) collective-permute-start(bf16[48,128]{1,0:T(8,128)(2,1)S(1)} %get-tuple-element.31), channel_id=1, source_target_pairs={{0,8},{8,0},{16,24},{24,16},{1,9},{9,1},{17,25},{25,17},{2,10},{10... | collective-permute-start | bytes 36872 | tf_op jit(solution)/shard_map/ppermute | solution.py:450
